TPU v7x, 32 devices: a whole 2x2x4 slice. The times are simulated.
32 devices in a mesh: dp: 8 (over z, x), mp: 4 (over y, core).
Axes of the slice: x: 2, y: 2, z: 4, core: 2. Of those that a mesh axis runs over, the one named last changes fastest.
Arguments:
- x_in: bfloat16 [32768, 768], P(('dp', 'mp')), may hold values from -6 to 6
- segments: int32 [32, 1024], P(('dp', 'mp')), may hold values from 0 to 4, never falling along the last dimension, each value on 1 to 312 neighbouring positions
- targets: bfloat16 [32768, 1024], P(('dp', 'mp')), may hold values from -6 to 6
- cotangent: bfloat16 [32768, 768], P(('dp', 'mp')), may hold values from -6 to 6
- norm_gain: float32 [3, 768], replicated, may hold values from 0.5 to 1.5
- norm_bias: float32 [3, 768], replicated, may hold values from -1.5 to 1.5
- attn_w: float32 [768, 4096], P(('dp', 'mp'))
- mlp_w: float32 [2, 768, 3072], P(None, 'dp', 'mp'), may hold values from -0.21875 to 0.21875
- norm_first: float32 [6, 768], replicated, may hold values from -128 to 128
- norm_second: float32 [6, 768], replicated, may hold values from 32.768 to 131.072
- attn_first: float32 [768, 4096], P(('dp', 'mp')), may hold values from -128 to 128
- attn_second: float32 [768, 4096], P(('dp', 'mp')), may hold values from 32.768 to 131.072
- mlp_first: float32 [2, 768, 3072], P(None, 'dp', 'mp'), may hold values from -128 to 128
- mlp_second: float32 [2, 768, 3072], P(None, 'dp', 'mp'), may hold values from 32.768 to 131.072
Outputs:
- y_out: bfloat16 [32768, 768], P(('dp', 'mp'))
- x_grad: float32 [32768, 768], P(('dp', 'mp'))
- attn_new: float32 [768, 4096], P(('dp', 'mp'))
- attn_first_new: float32 [768, 4096], P(('dp', 'mp'))
- attn_second_new: float32 [768, 4096], P(('dp', 'mp'))
- mlp_new: float32 [2, 768, 3072], P(None, 'dp', 'mp')
- mlp_first_new: float32 [2, 768, 3072], P(None, 'dp', 'mp')
- mlp_second_new: float32 [2, 768, 3072], P(None, 'dp', 'mp')
- norm_new: float32 [6, 768], replicated
- norm_first_new: float32 [6, 768], replicated
- norm_second_new: float32 [6, 768], replicated
- lamb_norms: float32 [2, 5], replicated
Inputs may be any that keep to these rules, and one draw needn't show every extreme that they name: `segments`: each row is one device's tokens: a packed run of whole clips, ids never fall along the row, each clip has 1 to 312 tokens and one has exactly 312.
All inputs are finite; a program needn't handle non-finite values.
Results may differ from a plain program's by a relative error of at most 0.015.
Values may be sent and summed in bfloat16 or wider, within the bound.
A program may use at most 256 MiB of HBM per device.

v0:
```python
import jax
import jax.numpy as jnp
from jax import lax
from jax.sharding import PartitionSpec as P

D = 768
H = 12
HD = 64
TD = 1024
STEP = 10


eps_norm = 1e-06
beta_one = 0.9
beta_two = 0.999
eps_adam = 1e-06
decay_rate = 0.05
learn_rate = 0.3


def norm_forward(values, gain_row, shift_row):
    centre = values - jnp.mean(values, axis=-1, keepdims=True)
    inv_std = lax.rsqrt(jnp.mean(centre * centre, axis=-1, keepdims=True) + eps_norm)
    normed = centre * inv_std
    return (normed * gain_row + shift_row, normed, inv_std)


def norm_backward(grad_norm, normed, inv_std, gain_row):
    scaled = grad_norm * gain_row
    centred = (
        scaled
        - jnp.mean(scaled, axis=-1, keepdims=True)
        - normed * jnp.mean(scaled * normed, axis=-1, keepdims=True)
    )
    return (centred * inv_std, jnp.sum(grad_norm * normed, axis=0), jnp.sum(grad_norm, axis=0))


def gelu_pair(pre_act):
    normal_cdf = 0.5 * (1.0 + jax.scipy.special.erf(pre_act * 0.7071067811865476))
    normal_pdf = jnp.exp(-0.5 * pre_act * pre_act) * 0.3989422804014327
    return (pre_act * normal_cdf, normal_cdf + pre_act * normal_pdf)


def split_heads(proj):
    tok_count = proj.shape[0]
    return (
        proj[:, :D].reshape(tok_count, H, HD),
        proj[:, D : 2 * D].reshape(tok_count, H, HD),
        proj[:, 2 * D :].reshape(tok_count, H, HD),
    )


def block_scores(queries, key_part, allowed):
    scores = jnp.einsum(
        "qhd,khd->hqk", queries, key_part, preferred_element_type=jnp.float32
    ) * HD ** (-0.5)
    return jnp.where(allowed[None], scores, -1e30)


def attention_forward(proj, allowed, block_rows):
    queries, key_part, value_part = split_heads(proj)
    pieces = []
    log_sums = []
    for offset in range(0, proj.shape[0], block_rows):
        scores = block_scores(
            queries[offset : offset + block_rows], key_part, allowed[offset : offset + block_rows]
        )
        row_max = jnp.max(scores, axis=-1, keepdims=True)
        exp_scores = jnp.exp(scores - row_max)
        row_total = jnp.sum(exp_scores, axis=-1, keepdims=True)
        attn_prob = (exp_scores / row_total).astype(jnp.bfloat16)
        context = jnp.einsum(
            "hqk,khd->qhd", attn_prob, value_part, preferred_element_type=jnp.float32
        )
        pieces.append(context.reshape(block_rows, D))
        log_sums.append(row_max + jnp.log(row_total))
    return (jnp.concatenate(pieces, axis=0), log_sums)


def attention_backward(proj, allowed, log_sums, grad_ctx, block_rows):
    queries, key_part, value_part = split_heads(proj)
    tok_count = proj.shape[0]
    grad_keys = jnp.zeros((tok_count, H, HD), jnp.float32)
    grad_vals = jnp.zeros((tok_count, H, HD), jnp.float32)
    grad_queries = []
    for block_idx, offset in enumerate(range(0, tok_count, block_rows)):
        query_block = queries[offset : offset + block_rows]
        scores = block_scores(query_block, key_part, allowed[offset : offset + block_rows])
        attn_prob = jnp.exp(scores - log_sums[block_idx])
        grad_block = grad_ctx[offset : offset + block_rows].reshape(block_rows, H, HD)
        grad_prob = jnp.einsum(
            "qhd,khd->hqk", grad_block, value_part, preferred_element_type=jnp.float32
        )
        delta = jnp.sum(grad_prob * attn_prob, axis=-1, keepdims=True)
        grad_score = (attn_prob * (grad_prob - delta)).astype(jnp.bfloat16)
        grad_queries.append(
            (
                jnp.einsum("hqk,khd->qhd", grad_score, key_part, preferred_element_type=jnp.float32)
                * HD ** (-0.5)
            ).reshape(block_rows, D)
        )
        grad_keys = grad_keys + jnp.einsum(
            "hqk,qhd->khd", grad_score, query_block, preferred_element_type=jnp.float32
        ) * HD ** (-0.5)
        grad_vals = grad_vals + jnp.einsum(
            "hqk,qhd->khd",
            attn_prob.astype(jnp.bfloat16),
            grad_block,
            preferred_element_type=jnp.float32,
        )
    return jnp.concatenate(
        [
            jnp.concatenate(grad_queries, axis=0),
            grad_keys.reshape(tok_count, D),
            grad_vals.reshape(tok_count, D),
        ],
        axis=1,
    )


def moments(weight, gradient, first_old, second_old, wd_rate):
    first_new = beta_one * first_old + (1.0 - beta_one) * gradient
    second_new = beta_two * second_old + (1.0 - beta_two) * gradient * gradient
    corr_one = 1.0 - beta_one**STEP
    corr_two = 1.0 - beta_two**STEP
    update = first_new / corr_one / (jnp.sqrt(second_new / corr_two) + eps_adam) + wd_rate * weight
    return (first_new, second_new, update)


def on_device(
    x_in,
    segments,
    targets,
    cotangent,
    norm_gain,
    norm_bias,
    attn_w,
    mlp_w,
    norm_first,
    norm_second,
    attn_first,
    attn_second,
    mlp_first,
    mlp_second,
):
    block_rows = min(512, x_in.shape[0])
    w_attn = lax.all_gather(attn_w.astype(jnp.bfloat16), ("dp", "mp"), axis=0, tiled=True)
    w_qkv = w_attn[:, : 3 * D]
    w_out = w_attn[:, 3 * D : 4 * D]
    w_head = w_attn[:, 4 * D :]
    w_mlp = lax.all_gather(mlp_w.astype(jnp.bfloat16), "dp", axis=1, tiled=True)
    residual = x_in.astype(jnp.float32)
    allowed = segments[0][:, None] == segments[0][None, :]
    norm_one, hat_one, inv_one = norm_forward(residual, norm_gain[0], norm_bias[0])
    h_one = norm_one.astype(jnp.bfloat16)
    proj = jnp.dot(h_one, w_qkv, preferred_element_type=jnp.float32).astype(jnp.bfloat16)
    context_raw, log_sums = attention_forward(proj, allowed, block_rows)
    context = context_raw.astype(jnp.bfloat16)
    middle = residual + jnp.dot(context, w_out, preferred_element_type=jnp.float32)
    norm_two, hat_two, inv_two = norm_forward(middle, norm_gain[1], norm_bias[1])
    h_two = norm_two.astype(jnp.bfloat16)
    w_full = lax.all_gather(w_mlp, "mp", axis=2, tiled=True)
    up_w = w_full[0]
    down_w = w_full[1]
    pre_act = jnp.dot(h_two, up_w, preferred_element_type=jnp.float32)
    activated, slope = gelu_pair(pre_act)
    hidden = activated.astype(jnp.bfloat16)
    partial_out = jnp.einsum("rf,df->rd", hidden, down_w, preferred_element_type=jnp.float32)
    block_out = middle + partial_out
    norm_three, hat_three, inv_three = norm_forward(block_out, norm_gain[2], norm_bias[2])
    h_three = norm_three.astype(jnp.bfloat16)
    aligned = jnp.dot(h_three, w_head, preferred_element_type=jnp.float32)
    teacher = targets.astype(jnp.float32)
    inv_al = lax.rsqrt(jnp.mean(aligned * aligned, axis=-1, keepdims=True) + eps_norm)
    inv_te = lax.rsqrt(jnp.mean(teacher * teacher, axis=-1, keepdims=True) + eps_norm)
    dot_mean = jnp.mean(aligned * teacher, axis=-1, keepdims=True)
    grad_al = (-(inv_al * inv_te) * (teacher - dot_mean * inv_al * inv_al * aligned)).astype(
        jnp.bfloat16
    )
    grad_head = jnp.einsum("td,ta->da", h_three, grad_al, preferred_element_type=jnp.float32)
    grad_h3 = jnp.einsum("ta,da->td", grad_al, w_head, preferred_element_type=jnp.float32)
    back_three, gain_three, bias_three = norm_backward(grad_h3, hat_three, inv_three, norm_gain[2])
    grad_out = cotangent.astype(jnp.float32) + back_three
    grad_out_low = grad_out.astype(jnp.bfloat16)
    grad_hidden = jnp.dot(grad_out_low, down_w, preferred_element_type=jnp.float32)
    grad_pre = (grad_hidden * slope).astype(jnp.bfloat16)
    grad_up = jnp.einsum("rd,rf->df", h_two, grad_pre, preferred_element_type=jnp.float32)
    grad_down = jnp.einsum("rd,rf->df", grad_out_low, hidden, preferred_element_type=jnp.float32)
    grad_h2_part = jnp.einsum("rf,df->rd", grad_pre, up_w, preferred_element_type=jnp.float32)
    grad_mlp = lax.psum_scatter(
        jnp.stack([grad_up, grad_down]).astype(jnp.bfloat16), "mp", scatter_dimension=2, tiled=True
    ).astype(jnp.float32)
    grad_mlp = lax.psum_scatter(grad_mlp, "dp", scatter_dimension=1, tiled=True)
    back_two, gain_two, bias_two = norm_backward(grad_h2_part, hat_two, inv_two, norm_gain[1])
    grad_mid = grad_out + back_two
    grad_mid_low = grad_mid.astype(jnp.bfloat16)
    grad_wout = jnp.einsum("tc,td->cd", context, grad_mid_low, preferred_element_type=jnp.float32)
    grad_ctx = jnp.einsum(
        "td,cd->tc", grad_mid_low, w_out, preferred_element_type=jnp.float32
    ).astype(jnp.bfloat16)
    grad_proj = attention_backward(proj, allowed, log_sums, grad_ctx, block_rows).astype(
        jnp.bfloat16
    )
    grad_wqkv = jnp.einsum("td,tc->dc", h_one, grad_proj, preferred_element_type=jnp.float32)
    grad_h1 = jnp.einsum("tc,dc->td", grad_proj, w_qkv, preferred_element_type=jnp.float32)
    back_one, gain_one, bias_one = norm_backward(grad_h1, hat_one, inv_one, norm_gain[0])
    grad_in = grad_mid + back_one
    local_small = jnp.stack([gain_one, gain_two, gain_three, bias_one, bias_two, bias_three])
    small_grad = lax.psum(local_small, ("dp", "mp"))
    grad_attn = lax.psum_scatter(
        jnp.concatenate([grad_wqkv, grad_wout, grad_head], axis=1),
        ("dp", "mp"),
        scatter_dimension=0,
        tiled=True,
    )
    attn_first_new, attn_second_new, attn_update = moments(
        attn_w, grad_attn, attn_first, attn_second, decay_rate
    )
    mlp_first_new, mlp_second_new, mlp_update = moments(
        mlp_w, grad_mlp, mlp_first, mlp_second, decay_rate
    )
    col_weight = jnp.sum(attn_w * attn_w, axis=0)
    col_update = jnp.sum(attn_update * attn_update, axis=0)
    weight_sq = jnp.stack(
        [
            jnp.sum(col_weight[: 3 * D]),
            jnp.sum(col_weight[3 * D : 4 * D]),
            jnp.sum(col_weight[4 * D :]),
            jnp.sum(mlp_w[0] * mlp_w[0]),
            jnp.sum(mlp_w[1] * mlp_w[1]),
        ]
    )
    update_sq = jnp.stack(
        [
            jnp.sum(col_update[: 3 * D]),
            jnp.sum(col_update[3 * D : 4 * D]),
            jnp.sum(col_update[4 * D :]),
            jnp.sum(mlp_update[0] * mlp_update[0]),
            jnp.sum(mlp_update[1] * mlp_update[1]),
        ]
    )
    local_stats = jnp.stack([weight_sq, update_sq])
    totals = lax.psum(local_stats, ("dp", "mp"))
    lamb_norms = jnp.sqrt(totals)
    ratio = lamb_norms[0] / lamb_norms[1]
    ratio_cols = jnp.concatenate(
        [jnp.full((3 * D,), ratio[0]), jnp.full((D,), ratio[1]), jnp.full((TD,), ratio[2])]
    )
    attn_new = attn_w - learn_rate * ratio_cols[None, :] * attn_update
    mlp_new = mlp_w - learn_rate * ratio[3:5][:, None, None] * mlp_update
    norm_w = jnp.concatenate([norm_gain, norm_bias], axis=0)
    norm_first_new, norm_second_new, norm_update = moments(
        norm_w, small_grad, norm_first, norm_second, 0.0
    )
    norm_ratio = jnp.sqrt(jnp.sum(norm_w * norm_w)) / jnp.sqrt(jnp.sum(norm_update * norm_update))
    norm_new = norm_w - learn_rate * norm_ratio * norm_update
    return (
        block_out.astype(jnp.bfloat16),
        grad_in,
        attn_new,
        attn_first_new,
        attn_second_new,
        mlp_new,
        mlp_first_new,
        mlp_second_new,
        norm_new,
        norm_first_new,
        norm_second_new,
        lamb_norms,
    )


def solution(mesh):
    placed = (
        P(("dp", "mp"), None),
        P(("dp", "mp"), None),
        P(("dp", "mp"), None),
        P(("dp", "mp"), None),
        P(),
        P(),
        P(("dp", "mp"), None),
        P(None, "dp", "mp"),
        P(),
        P(),
        P(("dp", "mp"), None),
        P(("dp", "mp"), None),
        P(None, "dp", "mp"),
        P(None, "dp", "mp"),
    )
    return jax.shard_map(
        on_device,
        mesh=mesh,
        in_specs=placed,
        out_specs=(
            P(("dp", "mp"), None),
            P(("dp", "mp"), None),
            P(("dp", "mp"), None),
            P(("dp", "mp"), None),
            P(("dp", "mp"), None),
            P(None, "dp", "mp"),
            P(None, "dp", "mp"),
            P(None, "dp", "mp"),
            P(),
            P(),
            P(),
            P(),
        ),
        check_vma=False,
    )
```

profile of v0, /device:TPU:0, one launch (start us, length us, event | category | flops | bytes accessed | tf_op | source)
XLA Modules:
  0.0 795.5 jit_solution(11611282482975599412)
XLA Ops:
  21.5 43.9 %all-gather.6.cloned.1.call-done = bf16[2,768,768]{2,1,0:T(8,128)(2,1)} async-done(((bf16[2,96,768]{2,1,0:T(8,128)(2,1)}), bf16[2,768,768]{2,1,0:T(8,128)(2,1)}) %all-gather.6.cloned.1.call-update) | async-done | bytes 2359312 | tf_op jit(solution)/shard_map/all_gather | solution.py:151
  65.6 71.0 %all-gather.4.cloned.1.call-done = bf16[768,4096]{1,0:T(8,128)(2,1)} async-done(((bf16[24,4096]{1,0:T(8,128)(2,1)}), bf16[768,4096]{1,0:T(8,128)(2,1)}) %all-gather.4.cloned.1.call-update) | async-done | bytes 6291472 | tf_op jit(solution)/shard_map/all_gather | solution.py:147
  136.6 6.4 convolution_convert_fusion
  155.9 12.1 %fusion.19 = (f32[12,512]{1,0:T(8,128)S(1)}, f32[12,512,1024]{2,1,0:T(8,128)}) fusion(pred[512,1024]{1,0:T(8,128)(4,1)} %get-tuple-element.80, bf16[512,12,64]{0,2,1:T(8,128)(2,1)} %bitcast.96, bf16[1024,12,64]{0,2,1:T(8,128)(2,1)S(1)} %bitcast.88), kind=kOutput, calls=%fused_computation.34 | convolution fusion | flops 824174592 | bytes 28073984 | tf_op jit(solution)/shard_map/qhd,khd->hqk/dot_general | solution.py:54
  168.0 10.8 %fusion.18 = (f32[12,512]{1,0:T(8,128)S(1)}, f32[12,512,1024]{2,1,0:T(8,128)}) fusion(pred[512,1024]{1,0:T(8,128)(4,1)S(1)} %copy-done.13, bf16[512,12,64]{0,2,1:T(8,128)(2,1)S(1)} %bitcast.98, bf16[1024,12,64]{0,2,1:T(8,128)(2,1)S(1)} %bitcast.89), kind=kOutput, calls=%fused_computation.33 | convolution fusion | flops 824174592 | bytes 28073984 | tf_op jit(solution)/shard_map/qhd,khd->hqk/dot_general | solution.py:54
  178.8 13.5 %fusion.1 = f32[12,512]{1,0:T(8,128)S(1)} fusion(f32[12,512]{1,0:T(8,128)S(1)} %get-tuple-element.87, f32[12,512,1024]{2,1,0:T(8,128)} %get-tuple-element.88, pred[512,1024]{1,0:T(8,128)(4,1)S(1)} %copy-done.17), kind=kLoop, calls=%fused_computation.13 | loop fusion | flops 25159680 | bytes 25739264 | tf_op jit(solution)/shard_map/reduce_sum | solution.py:70
  194.4 7.3 fusion
  201.7 12.9 %fusion.49 = bf16[12,64,512]{2,1,0:T(8,128)(2,1)} fusion(bf16[1024,12,64]{0,2,1:T(8,128)(2,1)S(1)} %bitcast.93, f32[12,512]{1,0:T(8,128)S(1)} %fusion.1, f32[12,512]{1,0:T(8,128)S(1)} %get-tuple-element.87, f32[12,512,1024]{2,1,0:T(8,128)} %get-tuple-element.88, pred[512,1024]{1,0:T(8,128)(4,1)S(1)} %copy-done.18), kind=kOutput, calls=%fused_computation.97 | convolution fusion | flops 837156864 | bytes 28098560 | tf_op jit(solution)/shard_map/hqk,khd->qhd/dot_general | solution.py:72
  214.7 8.5 %fusion.50 = bf16[12,64,512]{2,1,0:T(8,128)(2,1)} fusion(bf16[1024,12,64]{0,2,1:T(8,128)(2,1)S(1)} %bitcast.94, f32[12,512]{1,0:T(8,128)S(1)} %fusion, f32[12,512]{1,0:T(8,128)S(1)} %get-tuple-element.89, f32[12,512,1024]{2,1,0:T(8,128)S(1)} %copy-done, pred[512,1024]{1,0:T(8,128)(4,1)S(1)} %copy-done.14), kind=kOutput, calls=%fused_computation.98 | convolution fusion | flops 837156864 | bytes 28098560 | tf_op jit(solution)/shard_map/hqk,khd->qhd/dot_general | solution.py:72
  228.4 12.7 %multiply_convert_fusion.2 = (bf16[1024,3072]{1,0:T(8,128)(2,1)S(1)}, f32[1024,3072]{1,0:T(8,128)}) fusion(bf16[2,768,3072]{2,1,0:T(8,128)(2,1)} %all-gather.8.cloned.1.call-done, f32[1024,768]{0,1:T(8,128)} %copy-done.4, f32[768]{0:T(1024)S(1)} %copy-done.59, f32[768]{0:T(1024)S(1)} %copy-done.52, f32[1024]{0:T(1024)S(1)} %add_rsqrt_fusion.2, ...), kind=kOutput, calls=%fused_computation.28 | convolution fusion | flops 4851499008 | bytes 26753024 | tf_op jit(solution)/shard_map/dot_general | solution.py:165
  241.2 5.1 fusion.92
  260.5 4.6 multiply_reduce_fusion.3
  269.2 10.7 %fusion.21 = bf16[1,768,3072]{2,1,0:T(8,128)(2,1)} fusion(bf16[1024,3072]{1,0:T(8,128)(2,1)} %copy-done.67, f32[1024,768]{0,1:T(8,128)S(1)} %get-tuple-element.75), kind=kOutput, calls=%fused_computation.48 | convolution fusion | flops 4834983936 | bytes 14155776 | tf_op jit(solution)/shard_map/rd,rf->df/dot_general | solution.py:188
  279.9 12.4 %fusion.9 = bf16[1024,3072]{1,0:T(8,128)(2,1)S(1)} fusion(f32[1024,3072]{1,0:T(8,128)} %get-tuple-element.94, bf16[2,768,3072]{2,1,0:T(8,128)(2,1)S(1)} %bitcast.114, f32[1024,768]{0,1:T(8,128)S(1)} %get-tuple-element.75), kind=kOutput, calls=%fused_computation.22 | convolution fusion | flops 4864081920 | bytes 26738688 | tf_op jit(solution)/shard_map/dot_general | solution.py:185
  295.1 7.0 fusion.20
  302.2 8.2 %pad_maximum_fusion.1 = bf16[2,768,3072]{2,1,0:T(8,128)(2,1)} fusion(bf16[1,768,3072]{2,1,0:T(8,128)(2,1)} %fusion.21, bf16[1,768,3072]{2,1,0:T(8,128)(2,1)} %fusion.20), kind=kLoop, calls=%fused_computation.32 | loop fusion | flops 4718592 | bytes 18874368 | tf_op jit(solution)/shard_map/stack | solution.py:191
  310.4 10.0 %fusion.94 = (f32[768]{0:T(1024)S(1)}, f32[1024,768]{1,0:T(8,128)}) fusion(bf16[1024,3072]{1,0:T(8,128)(2,1)} %copy-done.68, bf16[2,768,3072]{2,1,0:T(8,128)(2,1)} %all-gather.8.cloned.1.call-done), kind=kOutput, calls=%fused_computation.191 | convolution fusion | flops 4832623616 | bytes 14158848 | tf_op jit(solution)/shard_map/rf,df->rd/dot_general | solution.py:189
  342.5 21.8 %multiply_reduce_fusion.1 = (f32[12,512]{1,0:T(8,128)S(1)}, f32[12,512,1024]{2,1,0:T(8,128)}) fusion(f32[12,512]{1,0:T(8,128)S(1)} %log_add_fusion.1, f32[12,512,1024]{2,1,0:T(8,128)} %get-tuple-element.90, pred[512,1024]{1,0:T(8,128)(4,1)S(1)} %copy-done.15, bf16[512,12,64]{0,2,1:T(8,128)(2,1)S(1)} %bitcast.102, bf16[1024,12,64]{0,2,1:T(8,128)(2,1)S(1)} %bitcast.95), kind=kOutput, calls=%fused_computation.4 | convolution fusion | flops 836757504 | bytes 53264384 | tf_op jit(solution)/shard_map/qhd,khd->hqk/dot_general | solution.py:91
  364.3 17.8 %multiply_convert_fusion.1 = bf16[12,512,1024]{2,1,0:T(8,128)(2,1)S(1)} fusion(f32[12,512,1024]{2,1,0:T(8,128)} %get-tuple-element.99, f32[12,512]{1,0:T(8,128)S(1)} %get-tuple-element.98, f32[12,512]{1,0:T(8,128)S(1)} %log_add_fusion.1, f32[12,512,1024]{2,1,0:T(8,128)} %get-tuple-element.90, pred[512,1024]{1,0:T(8,128)(4,1)} %get-tuple-element.79), kind=kLoop, calls=%fused_computation.3 | loop fusion | flops 37748736 | bytes 63488000 | tf_op jit(solution)/shard_map/convert_element_type | solution.py:95
  386.2 6.3 multiply_convert_fusion.5
  392.5 18.2 %multiply_reduce_fusion = (f32[12,512]{1,0:T(8,128)S(1)}, f32[12,512,1024]{2,1,0:T(8,128)}) fusion(f32[12,512]{1,0:T(8,128)S(1)} %log_add_fusion, f32[12,512,1024]{2,1,0:T(8,128)} %get-tuple-element.88, pred[512,1024]{1,0:T(8,128)(4,1)} %get-tuple-element.80, bf16[512,12,64]{0,2,1:T(8,128)(2,1)} %bitcast.104, bf16[1024,12,64]{0,2,1:T(8,128)(2,1)} %bitcast.92), kind=kOutput, calls=%fused_computation.1 | convolution fusion | flops 836757504 | bytes 53264384 | tf_op jit(solution)/shard_map/qhd,khd->hqk/dot_general | solution.py:91
  410.7 17.5 %multiply_convert_fusion = bf16[12,512,1024]{2,1,0:T(8,128)(2,1)S(1)} fusion(f32[12,512,1024]{2,1,0:T(8,128)} %get-tuple-element.101, f32[12,512]{1,0:T(8,128)S(1)} %get-tuple-element.100, f32[12,512]{1,0:T(8,128)S(1)} %log_add_fusion, f32[12,512,1024]{2,1,0:T(8,128)} %get-tuple-element.88, pred[512,1024]{1,0:T(8,128)(4,1)} %get-tuple-element.80), kind=kLoop, calls=%fused_computation | loop fusion | flops 37748736 | bytes 63488000 | tf_op jit(solution)/shard_map/convert_element_type | solution.py:95
  428.2 6.2 multiply_convert_fusion.4
  434.4 5.7 multiply_convert_fusion.3
  440.1 11.5 %fusion.10 = f32[12,64,1024]{2,1,0:T(8,128)S(1)} fusion(bf16[512,12,64]{0,2,1:T(8,128)(2,1)S(1)} %bitcast.105, f32[12,512]{1,0:T(8,128)S(1)} %log_add_fusion, f32[12,512,1024]{2,1,0:T(8,128)} %get-tuple-element.88, pred[512,1024]{1,0:T(8,128)(4,1)S(1)} %copy-done.19), kind=kOutput, calls=%fused_computation.23 | convolution fusion | flops 830472192 | bytes 29646848 | tf_op jit(solution)/shard_map/hqk,qhd->khd/dot_general | solution.py:105
  451.7 12.1 %add_convert_fusion = bf16[12,64,1024]{2,1,0:T(8,128)(2,1)S(1)} fusion(f32[12,64,1024]{2,1,0:T(8,128)S(1)} %fusion.10, bf16[512,12,64]{0,2,1:T(8,128)(2,1)S(1)} %bitcast.103, f32[12,512]{1,0:T(8,128)S(1)} %log_add_fusion.1, f32[12,512,1024]{2,1,0:T(8,128)} %get-tuple-element.90, pred[512,1024]{1,0:T(8,128)(4,1)S(1)} %copy-done.16), kind=kOutput, calls=%fused_computation.73 | convolution fusion | flops 832045056 | bytes 31219712 | tf_op jit(solution)/shard_map/hqk,qhd->khd/dot_general | solution.py:105
  468.1 5.0 pad_maximum_fusion
  481.9 8.9 %fusion.93 = (f32[768]{0:T(1024)S(1)}, f32[1024,768]{1,0:T(8,128)}) fusion(bf16[768,4096]{1,0:T(8,128)(2,1)} %all-gather.4.cloned.1.call-done, bf16[1024,768]{0,1:T(8,128)(2,1)} %bitcast.118, bf16[1024,768]{0,1:T(8,128)(2,1)S(1)} %bitcast.101, bf16[512,768]{0,1:T(8,128)(2,1)} %bitcast.108, bf16[512,768]{0,1:T(8,128)(2,1)} %bitcast.106), kind=kOutput, calls=%fused_computation.190 | convolution fusion | flops 3643538688 | bytes 11406336 | tf_op jit(solution)/shard_map/tc,dc->td/dot_general | solution.py:205
  498.3 5.9 fusion.40
  504.1 123.8 %reduce-scatter.4.cloned.1.call-done = f32[24,4096]{1,0:T(8,128)} async-done(((f32[768,4096]{1,0:T(8,128)}), f32[24,4096]{1,0:T(8,128)}) %reduce-scatter.4.cloned.1.call-update) | async-done | bytes 393232 | tf_op jit(solution)/shard_map/reduce_scatter | solution.py:210
  637.9 88.2 %reduce-scatter.8.cloned.1.call-done = f32[2,96,768]{2,1,0:T(8,128)} async-done(((f32[2,768,768]{2,1,0:T(8,128)}), f32[2,96,768]{2,1,0:T(8,128)}) %reduce-scatter.8.cloned.1.call-update) | async-done | bytes 589840 | tf_op jit(solution)/shard_map/reduce_scatter | solution.py:193
  736.2 40.5 %all-reduce = (f32[2,5]{1,0:T(2,128)S(1)}, f32[6,768]{1,0:T(8,128)S(1)}) all-reduce(f32[2,5]{1,0:T(2,128)S(1)} %pad_maximum_fusion.9, f32[6,768]{1,0:T(8,128)} %stack.102), channel_id=1, replica_groups=mesh['dp'=8,'mp'=4] {'dp','mp'}, use_global_device_ids=true, to_apply=%region_36.37 | all-reduce | flops 4618 | bytes 36944 | tf_op jit(solution)/shard_map/psum | solution.py:243
  (249 shorter events, 132.4 us)
Async XLA Ops:
  7.2 58.2 %all-gather.6.cloned.1.call-start = ((), (), s32[]{:S(2)}) async-start(), calls=%async_computation.4 | async-start | bytes 2654208 | tf_op jit(solution)/shard_map/all_gather | solution.py:151
  9.2 127.4 %all-gather.4.cloned.1.call-start = ((), (), s32[]{:S(2)}) async-start(), calls=%async_computation.3 | async-start | bytes 6488064 | tf_op jit(solution)/shard_map/all_gather | solution.py:147
  10.9 217.4 %all-gather.8.cloned.1.call-start = ((), (), s32[]{:S(2)}) async-start(), calls=%async_computation.5 | async-start | bytes 11796480 | tf_op jit(solution)/shard_map/all_gather | solution.py:162
  12.7 210.5 %copy-start.1 = (bf16[1024,768]{0,1:T(8,128)(2,1)}, bf16[1024,768]{0,1:T(8,128)(2,1)S(1)}, u32[]{:S(2)}) copy-start(bf16[1024,768]{0,1:T(8,128)(2,1)S(1)} %copy.50) | copy-start | bytes 4718596
  19.0 117.6 %copy-start.49 = (f32[768]{0:T(1024)}, f32[768]{0:T(1024)S(1)}, u32[]{:S(2)}) copy-start(f32[768]{0:T(1024)S(1)} %get-tuple-element.108) | copy-start | bytes 9220
  19.0 117.6 %copy-start.56 = (f32[768]{0:T(1024)}, f32[768]{0:T(1024)S(1)}, u32[]{:S(2)}) copy-start(f32[768]{0:T(1024)S(1)} %get-tuple-element.59) | copy-start | bytes 9220
  19.3 117.4 %copy-start.45 = (f32[1024]{0:T(1024)}, f32[1024]{0:T(1024)S(1)}, u32[]{:S(2)}) copy-start(f32[1024]{0:T(1024)S(1)} %broadcast_multiply_fusion.8) | copy-start | bytes 12292
  19.7 123.3 %copy-start.47 = (f32[1024]{0:T(1024)}, f32[1024]{0:T(1024)S(1)}, u32[]{:S(2)}) copy-start(f32[1024]{0:T(1024)S(1)} %add_rsqrt_fusion.3) | copy-start | bytes 12292
  65.4 407.8 %reduce-scatter.6.cloned.1.call-start = ((), (), s32[]{:S(2)}) async-start(), calls=%async_computation.7 | async-start | bytes 11796480 | tf_op jit(solution)/shard_map/reduce_scatter | solution.py:190
  148.1 19.9 %copy-start.3 = (bf16[1024,768]{0,1:T(8,128)(2,1)}, bf16[1024,768]{0,1:T(8,128)(2,1)S(1)}, u32[]{:S(2)}) copy-start(bf16[1024,768]{0,1:T(8,128)(2,1)S(1)} %copy.53) | copy-start | bytes 4718596
  155.9 12.1 %copy-start.25 = (bf16[512,768]{0,1:T(8,128)(2,1)S(1)}, bf16[512,768]{0,1:T(8,128)(2,1)}, u32[]{:S(2)}) copy-start(bf16[512,768]{0,1:T(8,128)(2,1)} %copy.52) | copy-start | bytes 2359300
  178.8 15.6 %copy-start = (f32[12,512,1024]{2,1,0:T(8,128)S(1)}, f32[12,512,1024]{2,1,0:T(8,128)}, u32[]{:S(2)}) copy-start(f32[12,512,1024]{2,1,0:T(8,128)} %get-tuple-element.90) | copy-start | bytes 75497472
  178.8 15.6 %copy-start.14 = (pred[512,1024]{1,0:T(8,128)(4,1)S(1)}, pred[512,1024]{1,0:T(8,128)(4,1)}, u32[]{:S(2)}) copy-start(pred[512,1024]{1,0:T(8,128)(4,1)} %get-tuple-element.79) | copy-start | bytes 1572868
  228.4 12.8 %copy-start.5 = (f32[1024,768]{0,1:T(8,128)S(1)}, f32[1024,768]{0,1:T(8,128)}, u32[]{:S(2)}) copy-start(f32[1024,768]{0,1:T(8,128)} %copy-done.4) | copy-start | bytes 9437188
  228.4 12.8 %copy-start.62 = (bf16[2,768,3072]{2,1,0:T(8,128)(2,1)S(1)}, bf16[2,768,3072]{2,1,0:T(8,128)(2,1)}, u32[]{:S(2)}) copy-start(bf16[2,768,3072]{2,1,0:T(8,128)(2,1)} %all-gather.8.cloned.1.call-done) | copy-start | bytes 28311556
  265.2 14.7 %slice-start = ((s8[9437184]{0:T(1024)(128)(4,1)}), s8[1048576]{0:T(1024)(128)(4,1)S(1)}, s32[]{:S(2)}) async-start(s8[9437184]{0:T(1024)(128)(4,1)} %bitcast.113), calls=%async_computation.9 | async-start | bytes 2097152
  265.2 14.7 %slice-start.1 = ((s8[9437184]{0:T(1024)(128)(4,1)}), s8[4194304]{0:T(1024)(128)(4,1)S(1)}, s32[]{:S(2)}) async-start(s8[9437184]{0:T(1024)(128)(4,1)} %bitcast.113), calls=%async_computation.10 | async-start | bytes 8388608
  310.4 317.5 %reduce-scatter.4.cloned.1.call-start = ((), (), s32[]{:S(2)}) async-start(), calls=%async_computation.6 | async-start | bytes 12976128 | tf_op jit(solution)/shard_map/reduce_scatter | solution.py:210
  364.3 17.8 %copy-start.26 = (bf16[512,768]{0,1:T(8,128)(2,1)S(1)}, bf16[512,768]{0,1:T(8,128)(2,1)}, u32[]{:S(2)}) copy-start(bf16[512,768]{0,1:T(8,128)(2,1)} %copy.52) | copy-start | bytes 2359300
  451.7 12.2 %copy-start.2 = (bf16[1024,768]{0,1:T(8,128)(2,1)S(1)}, bf16[1024,768]{0,1:T(8,128)(2,1)}, u32[]{:S(2)}) copy-start(bf16[1024,768]{0,1:T(8,128)(2,1)} %copy-done.1) | copy-start | bytes 4718596
  451.7 12.2 %copy-start.29 = (bf16[12,64,1024]{2,1,0:T(8,128)(2,1)S(1)}, bf16[12,64,1024]{2,1,0:T(8,128)(2,1)}, u32[]{:S(2)}) copy-start(bf16[12,64,1024]{2,1,0:T(8,128)(2,1)} %multiply_convert_fusion.3) | copy-start | bytes 4718596
  451.7 12.2 %copy-start.40 = (bf16[12,64,512]{2,1,0:T(8,128)(2,1)S(1)}, bf16[12,64,512]{2,1,0:T(8,128)(2,1)}, u32[]{:S(2)}) copy-start(bf16[12,64,512]{2,1,0:T(8,128)(2,1)} %multiply_convert_fusion.5) | copy-start | bytes 2359300
  451.7 12.2 %copy-start.41 = (bf16[12,64,512]{2,1,0:T(8,128)(2,1)S(1)}, bf16[12,64,512]{2,1,0:T(8,128)(2,1)}, u32[]{:S(2)}) copy-start(bf16[12,64,512]{2,1,0:T(8,128)(2,1)} %multiply_convert_fusion.4) | copy-start | bytes 2359300
  451.7 12.2 %copy-start.46 = (f32[1024]{0:T(1024)S(1)}, f32[1024]{0:T(1024)}, u32[]{:S(2)}) copy-start(f32[1024]{0:T(1024)} %copy-done.45) | copy-start | bytes 12292
  451.7 12.2 %copy-start.48 = (f32[1024]{0:T(1024)S(1)}, f32[1024]{0:T(1024)}, u32[]{:S(2)}) copy-start(f32[1024]{0:T(1024)} %copy-done.47) | copy-start | bytes 12292
  451.7 12.2 %copy-start.50 = (f32[768]{0:T(1024)S(1)}, f32[768]{0:T(1024)}, u32[]{:S(2)}) copy-start(f32[768]{0:T(1024)} %copy-done.49) | copy-start | bytes 9220
  451.7 12.2 %copy-start.57 = (f32[768]{0:T(1024)S(1)}, f32[768]{0:T(1024)}, u32[]{:S(2)}) copy-start(f32[768]{0:T(1024)} %copy-done.56) | copy-start | bytes 9220
  473.1 253.0 %reduce-scatter.8.cloned.1.call-start = ((), (), s32[]{:S(2)}) async-start(), calls=%async_computation.8 | async-start | bytes 5308416 | tf_op jit(solution)/shard_map/reduce_scatter | solution.py:193
  498.3 129.7 %copy-start.31 = (f32[24,4096]{1,0:T(8,128)S(1)}, f32[24,4096]{1,0:T(8,128)}, u32[]{:S(2)}) copy-start(f32[24,4096]{1,0:T(8,128)} %param.20) | copy-start | bytes 1179652
  504.1 229.7 %copy-start.20 = (f32[1024,768]{0,1:T(8,128)S(1)}, f32[1024,768]{0,1:T(8,128)}, u32[]{:S(2)}) copy-start(f32[1024,768]{0,1:T(8,128)} %fusion.40) | copy-start | bytes 9437188
  637.9 95.9 %copy-start.60 = (f32[5]{0:T(128)S(1)}, f32[5]{0:T(128)}, u32[]{:S(2)}) copy-start(f32[5]{0:T(128)} %stack.83) | copy-start | bytes 64
  733.8 45.9 %copy-start.43 = (f32[3,768]{1,0:T(4,128)S(1)}, f32[3,768]{1,0:T(4,128)}, u32[]{:S(2)}) copy-start(f32[3,768]{1,0:T(4,128)} %param.19) | copy-start | bytes 27652
  (48 other events, 244.5 us)
Sparse Core Ops, SparseCore 0:
  10.8 54.5 all-gather.5
  68.8 67.7 all-gather.3
  138.2 62.7 all-gather.7
  310.5 76.6 reduce-scatter.5
  473.2 154.6 reduce-scatter.3
  631.4 94.5 reduce-scatter.7
where the time goes:
time: 800 us; the launch traced here: 795 us
  waiting for transfers between devices  327 us (41%)
  matrix products  227 us (28%)
  other arithmetic  120 us (15%)
  local copies, waits for them, and re-layouts  63.5 us (8%)
  blocking collectives  40.5 us (5%)
  between operations  16.6 us (2%)
    reduce_scatter x1, waiting for transfers between devices, on_device(): lax.psum_scatter(jnp.concatenate([grad_wqkv, grad_wout, grad_head], axis=...  124 us
    reduce_scatter x1, waiting for transfers between devices, on_device(): grad_mlp = lax.psum_scatter(grad_mlp, 'dp', scatter_dimension=1, tiled=True)  88.2 us
    all_gather x1, waiting for transfers between devices, on_device(): lax.all_gather(attn_w.astype(jnp.bfloat16), ('dp', 'mp'), axis=0, tiled=T...  71 us
    all_gather x1, waiting for transfers between devices, on_device(): w_mlp = lax.all_gather(mlp_w.astype(jnp.bfloat16), 'dp', axis=1, tiled=True)  43.9 us
    psum x1, blocking collectives, on_device(): totals = lax.psum(local_stats, ('dp', 'mp'))  40.5 us
    dot_general x2, matrix products, attention_backward(): jnp.einsum('qhd,khd->hqk', grad_block, value_part, preferred_element_type...  40 us
    convert_element_type x2, other arithmetic, attention_backward(): grad_score = (attn_prob * (grad_prob - delta)).astype(jnp.bfloat16)  35.3 us
    unnamed x153, local copies, waits for them, and re-layouts  25.7 us
  transfers between devices with their start and end apart: 6, of which 4 were waited for; matrix products, arithmetic and copies ran while one was open for 38% of the time, Pallas kernels for 0%

commit v1 on v0

v1 whole, which is shorter than its diff:
```python
import functools
import jax
import jax.numpy as jnp
from jax import lax
from jax.experimental import pallas as pl
from jax.experimental.pallas import tpu as pltpu
from jax.sharding import PartitionSpec as P

D = 768
H = 12
HD = 64
FF = 3072
TD = 1024
T = 1024
LONGEST = 312
STEP = 10
QB = 128
TB = 256
FB = 768
GB = 512
F32 = jnp.float32
BF16 = jnp.bfloat16

eps_norm = 1e-06
beta_one = 0.9
beta_two = 0.999
eps_adam = 1e-06
decay_rate = 0.05
learn_rate = 0.3


def dot(a, b):
    return jnp.dot(a, b, preferred_element_type=F32)


def dot_t(a, b):
    return lax.dot_general(a, b, (((1,), (1,)), ((), ())), preferred_element_type=F32)


def norm_parts(values):
    centre = values - jnp.mean(values, axis=-1, keepdims=True)
    inv = lax.rsqrt(jnp.mean(centre * centre, axis=-1, keepdims=True) + eps_norm)
    return centre * inv, inv


def norm_back(grad, normed, inv, gain):
    scaled = grad * gain
    first = jnp.mean(scaled, axis=-1, keepdims=True)
    second = jnp.mean(scaled * normed, axis=-1, keepdims=True)
    return (scaled - first - normed * second) * inv


def window(block):
    low = max(0, (block * QB - (LONGEST - 1)) // QB * QB)
    high = min(T, -(-(block * QB + QB + LONGEST - 1) // QB) * QB)
    return low, high


def rows(index, size):
    return pl.ds(pl.multiple_of(index * size, size), size)


def compute_kernel(x_ref, seg_ref, gain_ref, shift_ref, tgt_hbm, cot_hbm, wa_hbm, wm_hbm,
                   y_hbm, xg_ref, ga_hbm, gm_hbm, small_ref,
                   wa, wm, gq, proj, h1t, ctxt, h2t, h3t, got, hid, gpre, tg, cot, ctx,
                   kaug, qaug, kt, vt, gka, gva, lse, delta, sem):
    loads = []
    for i, (src, dst) in enumerate(((wa_hbm, wa), (wm_hbm, wm), (tgt_hbm, tg), (cot_hbm, cot))):
        copy = pltpu.make_async_copy(src, dst, sem.at[i])
        copy.start()
        loads.append(copy)

    small_ref[...] = jnp.zeros_like(small_ref)
    marks = lax.broadcasted_iota(jnp.int32, (128, T), 0)
    same = jnp.where(marks == seg_ref[...], 1.0, 0.0).T
    kaug[:, 128:] = same.astype(BF16)
    lane = lax.broadcasted_iota(jnp.int32, (T, 128), 1)
    apart = jnp.where((lane < 8) & (same == 0.0), -1e30, 0.0).astype(BF16)
    for b in range(T // QB):
        for half in range(2):
            qaug[b * 2 * QB + half * QB:b * 2 * QB + (half + 1) * QB, 128:] = apart[b * QB:(b + 1) * QB]

    loads[0].wait()

    def first(i, _):
        r = rows(i, TB)
        hat, _inv = norm_parts(x_ref[r, :].astype(F32))
        h1 = (hat * gain_ref[0:1, :] + shift_ref[0:1, :]).astype(BF16)
        h1t[:, r] = h1.T
        proj[r, :] = dot(h1, wa[:, :3 * D]).astype(BF16)
        return 0

    lax.fori_loop(0, T // TB, first, 0)

    low_lane = lax.broadcasted_iota(jnp.int32, (QB, 128), 1) < HD
    low_row = lax.broadcasted_iota(jnp.int32, (128, QB), 0) < HD

    def slab(p, part):
        return pl.ds(pl.multiple_of(part * D + p * 128, 128), 128)

    def stage_pair(p):
        kaug[:, :128] = proj[:, slab(p, 1)]
        for b in range(T // QB):
            q = proj[b * QB:(b + 1) * QB, slab(p, 0)] * jnp.asarray(HD ** -0.5, BF16)
            qaug[b * 2 * QB:b * 2 * QB + QB, :128] = jnp.where(low_lane, q, jnp.zeros_like(q))
            qaug[b * 2 * QB + QB:(b + 1) * 2 * QB, :128] = jnp.where(low_lane, jnp.zeros_like(q), q)

    def attend(p, _):
        stage_pair(p)
        vt[...] = proj[:, slab(p, 2)].T
        for b in range(T // QB):
            low, high = window(b)
            s = dot_t(kaug[low:high, :], qaug[b * 2 * QB:(b + 1) * 2 * QB, :])
            top = jnp.max(s, axis=0, keepdims=True)
            e = jnp.exp(s - top)
            total = jnp.sum(e, axis=0, keepdims=True)
            r = dot(vt[:, low:high], e.astype(BF16)) / total
            c = jnp.where(low_row, r[:, :QB], r[:, QB:])
            lse[p, b:b + 1, :] = top + jnp.log(total)
            ctxt[pl.ds(pl.multiple_of(p * 128, 128), 128), b * QB:(b + 1) * QB] = c.astype(BF16)
            ctx[b * QB:(b + 1) * QB, slab(p, 0)] = c.T.astype(BF16)
        return 0

    lax.fori_loop(0, H // 2, attend, 0)
    loads[1].wait()

    def up(i, _):
        r = rows(i, TB)
        mid = x_ref[r, :].astype(F32) + dot(ctx[r, :], wa[:, 3 * D:4 * D])
        xg_ref[r, :] = mid
        hat, _inv = norm_parts(mid)
        h2 = (hat * gain_ref[1:2, :] + shift_ref[1:2, :]).astype(BF16)
        h2t[:, r] = h2.T

        for j in range(FF // FB):
            c = slice(j * FB, (j + 1) * FB)
            pre = dot(h2, wm[0, :, c])
            cdf = 0.5 * (1.0 + lax.erf(pre * 0.7071067811865476))
            pdf = jnp.exp(-0.5 * pre * pre) * 0.3989422804014327
            hid[r, c] = (pre * cdf).astype(BF16)
            gpre[r, c] = (cdf + pre * pdf).astype(BF16)
        return 0

    lax.fori_loop(0, T // TB, up, 0)
    loads[2].wait()
    loads[3].wait()
    head_of = (lax.broadcasted_iota(jnp.int32, (16, D), 1) // HD
               == lax.broadcasted_iota(jnp.int32, (16, D), 0)).astype(BF16)

    def down(i, _):
        r = rows(i, TB)
        mid = xg_ref[r, :]
        out = mid + dot_t(hid[r, :], wm[1])
        hat, inv = norm_parts(out)
        h3 = (hat * gain_ref[2:3, :] + shift_ref[2:3, :]).astype(BF16)
        h3t[:, r] = h3.T
        al = dot(h3, wa[:, 4 * D:])
        t = tg[r, :].astype(F32)
        ra = lax.rsqrt(jnp.mean(al * al, axis=-1, keepdims=True) + eps_norm)
        rt = lax.rsqrt(jnp.mean(t * t, axis=-1, keepdims=True) + eps_norm)
        c = jnp.mean(al * t, axis=-1, keepdims=True)
        gal = (-(ra * rt) * (t - c * ra * ra * al)).astype(BF16)
        tg[r, :] = gal
        g3 = dot_t(gal, wa[:, 4 * D:])
        small_ref[2:3, :] += jnp.sum(g3 * hat, axis=0, keepdims=True)
        small_ref[5:6, :] += jnp.sum(g3, axis=0, keepdims=True)
        gout = cot[r, :].astype(F32) + norm_back(g3, hat, inv, gain_ref[2:3, :])
        cot[r, :] = out.astype(BF16)
        low = gout.astype(BF16)
        got[:, r] = low.T
        for j in range(FF // FB):
            c = slice(j * FB, (j + 1) * FB)
            gpre[r, c] = (dot(low, wm[1, :, c]) * gpre[r, c].astype(F32)).astype(BF16)
        g2 = dot_t(gpre[r, :], wm[0])
        hat2, inv2 = norm_parts(mid)
        small_ref[1:2, :] += jnp.sum(g2 * hat2, axis=0, keepdims=True)
        small_ref[4:5, :] += jnp.sum(g2, axis=0, keepdims=True)
        gmid = gout + norm_back(g2, hat2, inv2, gain_ref[1:2, :])
        xg_ref[r, :] = gmid
        gc = dot_t(gmid.astype(BF16), wa[:, 3 * D:4 * D]).astype(BF16)
        e = ctx[r, :].astype(F32) * gc.astype(F32)
        e_high = e.astype(BF16)
        sums = dot_t(head_of, e_high) + dot_t(head_of, (e - e_high.astype(F32)).astype(BF16))
        for h in range(H):
            delta[h, :, r] = sums[h:h + 1, :]
        ctx[r, :] = gc
        return 0

    lax.fori_loop(0, T // TB, down, 0)
    y_copy = pltpu.make_async_copy(cot, y_hbm, sem.at[0])
    y_copy.start()

    wa[:, 4 * D:] = dot(h3t[...], tg[...]).astype(BF16)

    def ffgrad(j, _):
        c = rows(j, GB)
        wm[1, :, c] = dot(got[...], hid[:, c]).astype(BF16)
        wm[0, :, c] = dot(h2t[...], gpre[:, c]).astype(BF16)
        return 0

    lax.fori_loop(0, FF // GB, ffgrad, 0)
    wa[:, 3 * D:4 * D] = dot(ctxt[...], xg_ref[...].astype(BF16)).astype(BF16)

    def attend_back(p, _):
        stage_pair(p)
        kt[...] = proj[:, slab(p, 1)].T
        for b in range(T // QB):
            low, high = window(b)
            qs = slice(b * QB, (b + 1) * QB)
            q = qaug[b * 2 * QB:(b + 1) * 2 * QB, :]
            g = ctx[qs, slab(p, 0)]
            zero = jnp.zeros_like(g)
            g2 = jnp.concatenate([jnp.where(low_lane, g, zero), jnp.where(low_lane, zero, g)], axis=0)
            s = dot_t(kaug[low:high, :], q)
            prob = jnp.exp(s - lse[p, b:b + 1, :])
            dp = dot_t(proj[low:high, slab(p, 2)], g2)
            off = jnp.concatenate([delta[2 * p, :, qs], delta[2 * p + 1, :, qs]], axis=1)
            ds = (prob * (dp - off)).astype(BF16)
            pb = prob.astype(BF16)
            gk = dot(ds, q[:, :128])
            gv = dot(pb, g2)
            new = (0 if b == 0 else window(b - 1)[1])
            for lo, hi, fresh in ((low, min(new, high), False), (max(low, new), high, True)):
                if lo < hi:
                    a, z = lo - low, hi - low
                    gka[lo:hi, :] = gk[a:z] if fresh else gka[lo:hi, :] + gk[a:z]
                    gva[lo:hi, :] = gv[a:z] if fresh else gva[lo:hi, :] + gv[a:z]
            r = dot(kt[:, low:high], ds)
            c = jnp.where(low_row, r[:, :QB], r[:, QB:]) * HD ** -0.5
            proj[qs, slab(p, 0)] = c.T.astype(BF16)
        proj[:, slab(p, 1)] = gka[...].astype(BF16)
        proj[:, slab(p, 2)] = gva[...].astype(BF16)
        return 0

    lax.fori_loop(0, H // 2, attend_back, 0)

    for j in range(3):
        gq[:, j * D:(j + 1) * D] = dot(h1t[...], proj[:, j * D:(j + 1) * D]).astype(BF16)

    def last(i, _):
        r = rows(i, TB)
        g1 = dot_t(proj[r, :], wa[:, :3 * D])
        hat, inv = norm_parts(x_ref[r, :].astype(F32))
        small_ref[0:1, :] += jnp.sum(g1 * hat, axis=0, keepdims=True)
        small_ref[3:4, :] += jnp.sum(g1, axis=0, keepdims=True)
        xg_ref[r, :] += norm_back(g1, hat, inv, gain_ref[0:1, :])
        return 0

    lax.fori_loop(0, T // TB, last, 0)
    y_copy.wait()
    stores = []
    for i, (src, dst) in enumerate(((gq, ga_hbm.at[:, :3 * D]), (wa.at[:, 3 * D:], ga_hbm.at[:, 3 * D:]), (wm, gm_hbm))):
        copy = pltpu.make_async_copy(src, dst, sem.at[i])
        copy.start()
        stores.append(copy)
    for copy in stores:
        copy.wait()


def compute(x, seg, gain, shift, tgt, cot, wa, wm):
    vmem = pl.BlockSpec(memory_space=pltpu.VMEM)
    hbm = pl.BlockSpec(memory_space=pl.ANY)
    sds = jax.ShapeDtypeStruct
    return pl.pallas_call(
        compute_kernel,
        out_shape=(sds((T, D), BF16), sds((T, D), F32), sds((D, 4 * D + TD), BF16), sds((2, D, FF), BF16), sds((8, D), F32)),
        in_specs=[vmem, vmem, vmem, vmem, hbm, hbm, hbm, hbm],
        out_specs=(hbm, vmem, hbm, hbm, vmem),
        scratch_shapes=[
            pltpu.VMEM((D, 4 * D + TD), BF16), pltpu.VMEM((2, D, FF), BF16), pltpu.VMEM((D, 3 * D), BF16),
            pltpu.VMEM((T, 3 * D), BF16), pltpu.VMEM((D, T), BF16), pltpu.VMEM((D, T), BF16),
            pltpu.VMEM((D, T), BF16), pltpu.VMEM((D, T), BF16), pltpu.VMEM((D, T), BF16),
            pltpu.VMEM((T, FF), BF16), pltpu.VMEM((T, FF), BF16), pltpu.VMEM((T, TD), BF16),
            pltpu.VMEM((T, D), BF16), pltpu.VMEM((T, D), BF16),
            pltpu.VMEM((T, 256), BF16), pltpu.VMEM((2 * T, 256), BF16), pltpu.VMEM((128, T), BF16), pltpu.VMEM((128, T), BF16),
            pltpu.VMEM((T, 128), F32), pltpu.VMEM((T, 128), F32), pltpu.VMEM((H // 2, T // QB, 2 * QB), F32),
            pltpu.VMEM((H, 1, T), F32), pltpu.SemaphoreType.DMA((4,)),
        ],
        compiler_params=pltpu.CompilerParams(vmem_limit_bytes=67043328),
        name="block_step",
    )(x, seg, gain, shift, tgt, cot, wa, wm)


def moments(weight, gradient, first_old, second_old, wd_rate):
    first_new = beta_one * first_old + (1.0 - beta_one) * gradient
    second_new = beta_two * second_old + (1.0 - beta_two) * gradient * gradient
    corr_one = 1.0 - beta_one**STEP
    corr_two = 1.0 - beta_two**STEP
    update = first_new / corr_one / (jnp.sqrt(second_new / corr_two) + eps_adam) + wd_rate * weight
    return (first_new, second_new, update)


def on_device(
    x_in,
    segments,
    targets,
    cotangent,
    norm_gain,
    norm_bias,
    attn_w,
    mlp_w,
    norm_first,
    norm_second,
    attn_first,
    attn_second,
    mlp_first,
    mlp_second,
):
    w_attn = lax.all_gather(attn_w.astype(BF16), ("dp", "mp"), axis=0, tiled=True)
    w_mlp = lax.all_gather(mlp_w.astype(BF16), "dp", axis=1, tiled=True)
    w_mlp = lax.all_gather(w_mlp, "mp", axis=2, tiled=True)
    y_out, grad_in, part_attn, part_mlp, part_small = compute(
        x_in, segments, norm_gain, norm_bias, targets, cotangent, w_attn, w_mlp
    )
    grad_mlp = lax.psum_scatter(part_mlp, "dp", scatter_dimension=1, tiled=True)
    grad_mlp = lax.psum_scatter(grad_mlp, "mp", scatter_dimension=2, tiled=True).astype(F32)
    grad_attn = lax.psum_scatter(part_attn, ("dp", "mp"), scatter_dimension=0, tiled=True).astype(F32)
    small_grad = lax.psum(part_small[:6], ("dp", "mp"))
    attn_first_new, attn_second_new, attn_update = moments(
        attn_w, grad_attn, attn_first, attn_second, decay_rate
    )
    mlp_first_new, mlp_second_new, mlp_update = moments(
        mlp_w, grad_mlp, mlp_first, mlp_second, decay_rate
    )
    col_weight = jnp.sum(attn_w * attn_w, axis=0)
    col_update = jnp.sum(attn_update * attn_update, axis=0)
    weight_sq = jnp.stack(
        [
            jnp.sum(col_weight[: 3 * D]),
            jnp.sum(col_weight[3 * D : 4 * D]),
            jnp.sum(col_weight[4 * D :]),
            jnp.sum(mlp_w[0] * mlp_w[0]),
            jnp.sum(mlp_w[1] * mlp_w[1]),
        ]
    )
    update_sq = jnp.stack(
        [
            jnp.sum(col_update[: 3 * D]),
            jnp.sum(col_update[3 * D : 4 * D]),
            jnp.sum(col_update[4 * D :]),
            jnp.sum(mlp_update[0] * mlp_update[0]),
            jnp.sum(mlp_update[1] * mlp_update[1]),
        ]
    )
    local_stats = jnp.stack([weight_sq, update_sq])
    totals = lax.psum(local_stats, ("dp", "mp"))
    lamb_norms = jnp.sqrt(totals)
    ratio = lamb_norms[0] / lamb_norms[1]
    ratio_cols = jnp.concatenate(
        [jnp.full((3 * D,), ratio[0]), jnp.full((D,), ratio[1]), jnp.full((TD,), ratio[2])]
    )
    attn_new = attn_w - learn_rate * ratio_cols[None, :] * attn_update
    mlp_new = mlp_w - learn_rate * ratio[3:5][:, None, None] * mlp_update
    norm_w = jnp.concatenate([norm_gain, norm_bias], axis=0)
    norm_first_new, norm_second_new, norm_update = moments(
        norm_w, small_grad, norm_first, norm_second, 0.0
    )
    norm_ratio = jnp.sqrt(jnp.sum(norm_w * norm_w)) / jnp.sqrt(jnp.sum(norm_update * norm_update))
    norm_new = norm_w - learn_rate * norm_ratio * norm_update
    return (
        y_out,
        grad_in,
        attn_new,
        attn_first_new,
        attn_second_new,
        mlp_new,
        mlp_first_new,
        mlp_second_new,
        norm_new,
        norm_first_new,
        norm_second_new,
        lamb_norms,
    )


def solution(mesh):
    placed = (
        P(("dp", "mp"), None),
        P(("dp", "mp"), None),
        P(("dp", "mp"), None),
        P(("dp", "mp"), None),
        P(),
        P(),
        P(("dp", "mp"), None),
        P(None, "dp", "mp"),
        P(),
        P(),
        P(("dp", "mp"), None),
        P(("dp", "mp"), None),
        P(None, "dp", "mp"),
        P(None, "dp", "mp"),
    )
    return jax.shard_map(
        on_device,
        mesh=mesh,
        in_specs=placed,
        out_specs=(
            P(("dp", "mp"), None),
            P(("dp", "mp"), None),
            P(("dp", "mp"), None),
            P(("dp", "mp"), None),
            P(("dp", "mp"), None),
            P(None, "dp", "mp"),
            P(None, "dp", "mp"),
            P(None, "dp", "mp"),
            P(),
            P(),
            P(),
            P(),
        ),
        check_vma=False,
    )
```

time: 800 us -> 710 us (0.89)
  matrix products: 227 us -> 0 us
  waiting for transfers between devices: 327 us -> 491 us
  Pallas kernels: 0 us -> 137 us
  other arithmetic: 120 us -> 16 us
  local copies, waits for them, and re-layouts: 63.5 us -> 9.18 us
    dot_general x27 -> x0, matrix products: 227 us -> none  [the longest x2 40 us: attention_backward(): jnp.einsum('qhd,khd->hqk', grad_block, value_part, preferred_element_type...]
    pallas_call x0 -> x1, Pallas kernels: none -> 137 us  [compute(): pl.pallas_call(compute_kernel, out_shape=(sds((T, D), BF16), sds((T, D),...]
    reduce_scatter x3, waiting for transfers between devices: 212 us -> 301 us  [the longest x1 162 us: on_device(): grad_mlp = lax.psum_scatter(part_mlp, 'dp', scatter_dimension=1, tiled=True)]
    all_gather x3, waiting for transfers between devices: 115 us -> 190 us  [the longest x1 71.2 us: on_device(): lax.all_gather(attn_w.astype(BF16), ('dp', 'mp'), axis=0, tiled=True)]
    convert_element_type x6 -> x2, other arithmetic: 43.9 us -> 3.51 us  [the longest x1 1.81 us: on_device(): w_mlp = lax.all_gather(mlp_w.astype(BF16), 'dp', axis=1, tiled=True)]
    reduce_sum x12 -> x0, other arithmetic: 34.9 us -> none  [the longest x2 20.8 us: attention_forward(): row_total = jnp.sum(exp_scores, axis=-1, keepdims=True)]
    unnamed x153 -> x18, local copies, waits for them, and re-layouts: 25.7 us -> 0.06 us
    slice x9 -> x0, local copies, waits for them, and re-layouts: 15.5 us -> none  [the longest x3 6.48 us: attention_forward(): queries[offset:offset + block_rows]]
  transfers between devices with their start and end apart: 6 -> 6, of which waited for: 4 -> 6; matrix products, arithmetic and copies ran while one was open for 38% -> 1% of each run, Pallas kernels for 0% -> 0%
where the time goes in v1:
time: 710 us; the launch traced here: 709 us
  waiting for transfers between devices  491 us (69%)
  Pallas kernels  137 us (19%)
  blocking collectives  39.7 us (6%)
  other arithmetic  16 us (2%)
  between operations  15.7 us (2%)
  local copies, waits for them, and re-layouts  9.18 us (1%)
    reduce_scatter x1, waiting for transfers between devices, on_device(): grad_mlp = lax.psum_scatter(part_mlp, 'dp', scatter_dimension=1, tiled=True)  162 us
    pallas_call x1, Pallas kernels, compute(): pl.pallas_call(compute_kernel, out_shape=(sds((T, D), BF16), sds((T, D),...  137 us
    reduce_scatter x1, waiting for transfers between devices, on_device(): lax.psum_scatter(part_attn, ('dp', 'mp'), scatter_dimension=0, tiled=True)  119 us
    all_gather x1, waiting for transfers between devices, on_device(): lax.all_gather(attn_w.astype(BF16), ('dp', 'mp'), axis=0, tiled=True)  71.2 us
    all_gather x1, waiting for transfers between devices, on_device(): w_mlp = lax.all_gather(w_mlp, 'mp', axis=2, tiled=True)  64.3 us
    all_gather x1, waiting for transfers between devices, on_device(): w_mlp = lax.all_gather(mlp_w.astype(BF16), 'dp', axis=1, tiled=True)  54.5 us
    psum x1, blocking collectives, on_device(): totals = lax.psum(local_stats, ('dp', 'mp'))  39.7 us
    reduce_scatter x1, waiting for transfers between devices, on_device(): lax.psum_scatter(grad_mlp, 'mp', scatter_dimension=2, tiled=True)  20.3 us
  transfers between devices with their start and end apart: 6, of which 6 were waited for; matrix products, arithmetic and copies ran while one was open for 1% of the time, Pallas kernels for 0%

profile of v1, /device:TPU:0, one launch (start us, length us, event | category | flops | bytes accessed | tf_op | source)
XLA Modules:
  0.0 709.0 jit_solution(13340236867429623403)
XLA Ops:
  7.2 1.8 convert_element_type.13
  9.1 0.0 all-gather.4.cloned.1.call-start
  9.1 1.7 convert_element_type.12
  10.8 0.0 all-gather.8.cloned.1.call-start
  10.9 54.5 %all-gather.6.cloned.1.call-done = bf16[2,768,768]{2,1,0:T(8,128)(2,1)} async-done(((bf16[2,96,768]{2,1,0:T(8,128)(2,1)}), bf16[2,768,768]{2,1,0:T(8,128)(2,1)}) %all-gather.6.cloned.1.call-update) | async-done | bytes 2359312 | tf_op jit(solution)/shard_map/all_gather | solution.py:310
  65.4 71.2 %all-gather.4.cloned.1.call-done.wa_hbm = bf16[768,4096]{1,0:T(8,128)(2,1)} async-done(((bf16[24,4096]{1,0:T(8,128)(2,1)}), bf16[768,4096]{1,0:T(8,128)(2,1)}) %all-gather.4.cloned.1.call-update) | async-done | bytes 6291472 | tf_op jit(solution)/shard_map/all_gather | solution.py:309
  136.6 64.3 %all-gather.8.cloned.1.call-done.wm_hbm = bf16[2,768,3072]{2,1,0:T(8,128)(2,1)} async-done(((bf16[2,768,768]{2,1,0:T(8,128)(2,1)}), bf16[2,768,3072]{2,1,0:T(8,128)(2,1)}) %all-gather.8.cloned.1.call-update) | async-done | bytes 9437200 | tf_op jit(solution)/shard_map/all_gather | solution.py:311
  201.0 136.7 %block_step.1 = (bf16[1024,768]{1,0:T(8,128)(2,1)}, f32[1024,768]{1,0:T(8,128)}, bf16[768,4096]{1,0:T(8,128)(2,1)}, bf16[2,768,3072]{2,1,0:T(8,128)(2,1)}, f32[8,768]{1,0:T(8,128)}) custom-call(bf16[1024,768]{1,0:T(8,128)(2,1)} %x_ref.1, s32[1,1024]{1,0:T(1,128)} %seg_ref.1, f32[3,768]{1,0:T(4,128)} %gain_ref.1, f32[3,768]{1,0:T(4,128)} %shift_ref.1, ...), custom_call_target="tpu_custom_call" | custom-call | tf_op jit(solution)/shard_map/block_step/pallas_call | solution.py:264
  337.7 0.0 reduce-scatter.4.cloned.1.call-start
  337.8 0.5 reduce-scatter.4.cloned.1.call-update
  338.4 161.6 %reduce-scatter.6.cloned.1.call-done = bf16[2,96,3072]{2,1,0:T(8,128)(2,1)} async-done(((bf16[2,768,3072]{2,1,0:T(8,128)(2,1)}), bf16[2,96,3072]{2,1,0:T(8,128)(2,1)}) %reduce-scatter.6.cloned.1.call-update) | async-done | bytes 1179664 | tf_op jit(solution)/shard_map/reduce_scatter | solution.py:315
  500.1 0.7 multiply_reduce_fusion.2
  500.7 118.9 %reduce-scatter.4.cloned.1.call-done = bf16[24,4096]{1,0:T(8,128)(2,1)} async-done(((bf16[768,4096]{1,0:T(8,128)(2,1)}), bf16[24,4096]{1,0:T(8,128)(2,1)}) %reduce-scatter.4.cloned.1.call-update) | async-done | bytes 196624 | tf_op jit(solution)/shard_map/reduce_scatter | solution.py:317
  619.6 1.5 multiply_reduce_fusion.1
  621.2 0.7 slice_reduce_fusion.2
  621.9 0.6 slice_reduce_fusion.3
  622.5 0.6 slice_reduce_fusion
  623.1 3.2 stack.50
  626.4 20.3 %reduce-scatter.8.cloned.1.call-done = bf16[2,96,768]{2,1,0:T(8,128)(2,1)} async-done(((bf16[2,96,3072]{2,1,0:T(8,128)(2,1)}), bf16[2,96,768]{2,1,0:T(8,128)(2,1)}) %reduce-scatter.8.cloned.1.call-update) | async-done | bytes 294928 | tf_op jit(solution)/shard_map/reduce_scatter | solution.py:316
  646.7 2.4 multiply_add_fusion
  649.1 0.7 fusion.4
  649.7 3.3 stack.57
  653.1 39.7 %all-reduce = (f32[2,5]{1,0:T(2,128)S(1)}, f32[6,768]{1,0:T(8,128)S(1)}) all-reduce(f32[2,5]{1,0:T(2,128)S(1)} %pad_maximum_fusion.1, f32[6,768]{1,0:T(8,128)} %bitcast.18), channel_id=1, replica_groups=mesh['dp'=8,'mp'=4] {'dp','mp'}, use_global_device_ids=true, to_apply=%region_15.0 | all-reduce | flops 4618 | bytes 36944 | tf_op jit(solution)/shard_map/psum | solution.py:346
  692.8 0.1 multiply_bitcast_fusion
  692.9 0.7 fusion.12
  693.5 2.0 multiply_reduce_fusion.4
  696.9 0.9 multiply_subtract_fusion
  697.9 1.3 multiply_subtract_fusion.2
  699.2 0.6 broadcast_in_dim.11
  699.8 0.6 broadcast_in_dim.12
  700.4 0.7 broadcast_in_dim.13
  701.1 1.0 multiply_subtract_fusion.1
  (30 shorter events, 0.3 us)
Async XLA Ops:
  7.2 58.1 %all-gather.6.cloned.1.call-start = ((), (), s32[]{:S(2)}) async-start(), calls=%async_computation.4 | async-start | bytes 2654208 | tf_op jit(solution)/shard_map/all_gather | solution.py:310
  9.1 127.6 %all-gather.4.cloned.1.call-start = ((), (), s32[]{:S(2)}) async-start(), calls=%async_computation.3 | async-start | bytes 6488064 | tf_op jit(solution)/shard_map/all_gather | solution.py:309
  10.8 190.1 %all-gather.8.cloned.1.call-start = ((), (), s32[]{:S(2)}) async-start(), calls=%async_computation.5 | async-start | bytes 11796480 | tf_op jit(solution)/shard_map/all_gather | solution.py:311
  65.4 434.7 %reduce-scatter.6.cloned.1.call-start = ((), (), s32[]{:S(2)}) async-start(), calls=%async_computation.7 | async-start | bytes 10616832 | tf_op jit(solution)/shard_map/reduce_scatter | solution.py:315
  337.7 281.9 %reduce-scatter.4.cloned.1.call-start = ((), (), s32[]{:S(2)}) async-start(), calls=%async_computation.6 | async-start | bytes 6488064 | tf_op jit(solution)/shard_map/reduce_scatter | solution.py:317
  337.8 162.3 %copy-start = (f32[2,96,768]{2,1,0:T(8,128)S(1)}, f32[2,96,768]{2,1,0:T(8,128)}, u32[]{:S(2)}) copy-start(f32[2,96,768]{2,1,0:T(8,128)} %param.21) | copy-start | bytes 1769476
  337.8 281.8 %copy-start.1 = (f32[24,4096]{1,0:T(8,128)S(1)}, f32[24,4096]{1,0:T(8,128)}, u32[]{:S(2)}) copy-start(f32[24,4096]{1,0:T(8,128)} %param.20) | copy-start | bytes 1179652
  337.8 281.8 %copy-start.6 = (f32[24,4096]{1,0:T(8,128)S(1)}, f32[24,4096]{1,0:T(8,128)}, u32[]{:S(2)}) copy-start(f32[24,4096]{1,0:T(8,128)} %param.24) | copy-start | bytes 1179652
  338.3 308.3 %copy-start.4 = (f32[2,96,768]{2,1,0:T(8,128)S(1)}, f32[2,96,768]{2,1,0:T(8,128)}, u32[]{:S(2)}) copy-start(f32[2,96,768]{2,1,0:T(8,128)} %param.26) | copy-start | bytes 1769476
  338.3 308.3 %copy-start.5 = (f32[2,96,768]{2,1,0:T(8,128)S(1)}, f32[2,96,768]{2,1,0:T(8,128)}, u32[]{:S(2)}) copy-start(f32[2,96,768]{2,1,0:T(8,128)} %param.27) | copy-start | bytes 1769476
  338.4 308.3 %reduce-scatter.8.cloned.1.call-start = ((), (), s32[]{:S(2)}) async-start(), calls=%async_computation.8 | async-start | bytes 1474560 | tf_op jit(solution)/shard_map/reduce_scatter | solution.py:316
  621.2 80.0 %copy-start.2 = (f32[24,4096]{1,0:T(8,128)}, f32[24,4096]{1,0:T(8,128)S(1)}, u32[]{:S(2)}) copy-start(f32[24,4096]{1,0:T(8,128)S(1)} %get-tuple-element.37) | copy-start | bytes 1179652
  621.2 80.0 %copy-start.3 = (f32[24,4096]{1,0:T(8,128)}, f32[24,4096]{1,0:T(8,128)S(1)}, u32[]{:S(2)}) copy-start(f32[24,4096]{1,0:T(8,128)S(1)} %get-tuple-element.38) | copy-start | bytes 1179652
  621.2 72.3 %copy-start.7 = (f32[3,768]{1,0:T(4,128)S(1)}, f32[3,768]{1,0:T(4,128)}, u32[]{:S(2)}) copy-start(f32[3,768]{1,0:T(4,128)} %gain_ref.1) | copy-start | bytes 27652
  692.8 9.3 %copy-start.8 = (f32[2,5]{1,0:T(2,128)}, f32[2,5]{1,0:T(2,128)S(1)}, u32[]{:S(2)}) copy-start(f32[2,5]{1,0:T(2,128)S(1)} %sqrt.20) | copy-start | bytes 124
Sparse Core Ops, SparseCore 0:
  10.7 54.5 all-gather.5
  68.8 67.7 all-gather.3
  138.2 62.7 all-gather.7
  337.9 162.1 reduce-scatter.5
  505.5 114.0 reduce-scatter.3
  622.1 24.5 reduce-scatter.7

commit v2 on v1

--- a/solution.py
+++ b/solution.py
@@ -60,17 +60,158 @@
     return pl.ds(pl.multiple_of(index * size, size), size)
 
 
-def compute_kernel(x_ref, seg_ref, gain_ref, shift_ref, tgt_hbm, cot_hbm, wa_hbm, wm_hbm,
-                   y_hbm, xg_ref, ga_hbm, gm_hbm, small_ref,
-                   wa, wm, gq, proj, h1t, ctxt, h2t, h3t, got, hid, gpre, tg, cot, ctx,
-                   kaug, qaug, kt, vt, gka, gva, lse, delta, sem):
-    loads = []
-    for i, (src, dst) in enumerate(((wa_hbm, wa), (wm_hbm, wm), (tgt_hbm, tg), (cot_hbm, cot))):
-        copy = pltpu.make_async_copy(src, dst, sem.at[i])
+FIVE = (2, 2, 2, 2, 2)
+Z2, Z1, X, Y, C = range(5)
+ALL = slice(None)
+
+
+class Place:
+    def __init__(self):
+        dp, mp = lax.axis_index("dp"), lax.axis_index("mp")
+        self.mine = (lax.rem(lax.div(dp, 4), 2), lax.rem(lax.div(dp, 2), 2), lax.rem(dp, 2), lax.div(mp, 2), lax.rem(mp, 2))
+        self.dp, self.mp = dp, mp
+
+    def partner(self, bit):
+        turn = 1 - 2 * self.mine[bit]
+        if bit <= X:
+            return {"dp": self.dp + turn * (4, 2, 1)[bit], "mp": self.mp}
+        return {"dp": self.dp, "mp": self.mp + turn * (2, 1)[bit - Y]}
+
+
+class Piece:
+    def __init__(self, ref, lead, row, col):
+        self.ref, self.lead, self.row, self.col = ref, lead, row, col
+
+    def where(self, bits):
+        return (*self.lead, *bits, self.row, self.col)
+
+    def at(self, bits):
+        return self.ref.at[self.where(bits)]
+
+
+class Gather:
+    def __init__(self, place, piece, order, send, recv):
+        self.copies, self.step, self.live = [], -1, True
+        for j, bit in enumerate(order):
+            view = piece.at(tuple(ALL if d in order[:j] else place.mine[d] for d in range(5)))
+            self.copies.append(pltpu.make_async_remote_copy(
+                view, view, send.at[j], recv.at[j], device_id=place.partner(bit), device_id_type=pl.DeviceIdType.MESH))
+
+    def go(self):
+        if self.step >= 0:
+            self.copies[self.step].wait()
+        self.step += 1
+        if self.step < 5:
+            self.copies[self.step].start()
+
+    def finish(self):
+        while self.step < 5:
+            self.go()
+
+
+class Scatter:
+    def __init__(self, place, piece, order, lands, send, recv, out):
+        self.copies, self.step, self.out = [], -1, out
+        self.place, self.piece, self.order, self.lands = place, piece, order, lands
+        for j, bit in enumerate(order):
+            view = piece.at(tuple(1 - place.mine[d] if d == bit else place.mine[d] if d in order[:j] else ALL for d in range(5)))
+            land = lands[j].at((ALL,) * (4 - j))
+            self.copies.append(pltpu.make_async_remote_copy(
+                view, land, send.at[j], recv.at[j], device_id=place.partner(bit), device_id_type=pl.DeviceIdType.MESH))
+
+    def go(self):
+        if self.step >= 0:
+            j = self.step
+            self.copies[j].wait()
+            left = [d for d in range(5) if d not in self.order[:j + 1]]
+            piece, land, mine = self.piece, self.lands[j], self.place.mine
+
+            def add(i, _):
+                at = [lax.rem(lax.div(i, 2 ** (len(left) - 1 - k)), 2) for k in range(len(left))]
+                bits = tuple(at[left.index(d)] if d in left else mine[d] for d in range(5))
+                here, there = piece.where(bits), land.where(tuple(at))
+                if j == 4:
+                    self.out(piece.ref[here].astype(F32) + land.ref[there].astype(F32))
+                else:
+                    piece.ref[here] = piece.ref[here] + land.ref[there]
+                return 0
+
+            if left:
+                lax.fori_loop(0, 2 ** len(left), add, 0)
+            else:
+                add(0, 0)
+        self.step += 1
+        if self.step < 5:
+            self.copies[self.step].start()
+
+    def finish(self):
+        while self.step < 5:
+            self.go()
+
+
+class Total:
+    def __init__(self, place, ref, land, send, recv):
+        self.ref, self.land, self.step = ref, land, -1
+        self.copies = [pltpu.make_async_remote_copy(
+            ref, land.at[j], send.at[j], recv.at[j], device_id=place.partner(j), device_id_type=pl.DeviceIdType.MESH) for j in range(5)]
+
+    def go(self):
+        if self.step >= 0:
+            self.copies[self.step].wait()
+            self.ref[...] = self.ref[...] + self.land[self.step]
+        self.step += 1
+        if self.step < 5:
+            self.copies[self.step].start()
+
+
+def step_kernel(comm, *refs):
+    (x_ref, seg_ref, gain_ref, shift_ref, tgt_hbm, cot_hbm, wa_in, wm_in,
+     y_hbm, xg_ref, ga_out, gm_out, small_ref, *refs) = refs
+    (wa, wm, gq, proj, h1t, ctxt, h2t, h3t, got, hid, gpre, tg, cot, ctx,
+     kaug, qaug, kt, gka, gva, lse, delta, sem, *refs) = refs
+    everywhere = (ALL,) * 5
+
+    def wide(cols):
+        return wa[(*everywhere, ALL, cols)].reshape(D, -1)
+
+    def tall(m, j):
+        return wm[(m, ALL, ALL, ALL, j // 2, j % 2)].reshape(D, FB)
+
+    loads = [pltpu.make_async_copy(src, dst, sem.at[i]) for i, (src, dst) in enumerate(((tgt_hbm, tg), (cot_hbm, cot)))]
+    if not comm:
+        loads += [pltpu.make_async_copy(src, dst, sem.at[i + 2]) for i, (src, dst) in enumerate(((wa_in, wa), (wm_in, wm)))]
+    for copy in loads:
         copy.start()
-        loads.append(copy)
-
     small_ref[...] = jnp.zeros_like(small_ref)
+
+    qkv_cols, out_cols, head_cols = slice(0, 3 * D), slice(3 * D, 4 * D), slice(4 * D, 4 * D + TD)
+    half_a, half_b = slice(0, 9 * 128), slice(9 * 128, 3 * D)
+    if comm:
+        ag_send, ag_recv, rs_send, rs_recv, ready, sm_send, sm_recv, sm_land = refs
+        place = Place()
+        mine = place.mine
+        wa[(*mine, ALL, ALL)] = wa_in[...].astype(BF16)
+        for m in range(2):
+            wm[(m, *mine, ALL, ALL)] = wm_in[m].astype(BF16)
+        barrier = pltpu.get_barrier_semaphore()
+        for bit in range(5):
+            pl.semaphore_signal(barrier, inc=1, device_id=place.partner(bit), device_id_type=pl.DeviceIdType.MESH)
+        pl.semaphore_wait(barrier, 5)
+        xy, yx = (Z2, Z1, X, Y, C), (Z2, Z1, Y, X, C)
+
+        def gather(k, piece, order):
+            return Gather(place, piece, order, ag_send.at[k], ag_recv.at[k])
+
+        ag_a = gather(0, Piece(wa, (), ALL, half_a), xy)
+        ag_b = gather(1, Piece(wa, (), ALL, half_b), yx)
+        ag_out = gather(2, Piece(wa, (), ALL, out_cols), xy)
+        ag_up = gather(3, Piece(wm, (0,), ALL, ALL), xy)
+        ag_down = gather(4, Piece(wm, (1,), ALL, ALL), yx)
+        ag_head = gather(5, Piece(wa, (), ALL, head_cols), yx)
+        rest = (ag_up, ag_down, ag_out, ag_head)
+        ag_a.go()
+        ag_b.go()
+
     marks = lax.broadcasted_iota(jnp.int32, (128, T), 0)
     same = jnp.where(marks == seg_ref[...], 1.0, 0.0).T
     kaug[:, 128:] = same.astype(BF16)
@@ -80,14 +221,39 @@
         for half in range(2):
             qaug[b * 2 * QB + half * QB:b * 2 * QB + (half + 1) * QB, 128:] = apart[b * QB:(b + 1) * QB]
 
-    loads[0].wait()
-
-    def first(i, _):
+    def enter(i, _):
         r = rows(i, TB)
         hat, _inv = norm_parts(x_ref[r, :].astype(F32))
         h1 = (hat * gain_ref[0:1, :] + shift_ref[0:1, :]).astype(BF16)
         h1t[:, r] = h1.T
-        proj[r, :] = dot(h1, wa[:, :3 * D]).astype(BF16)
+        ctx[r, :] = h1
+        return 0
+
+    lax.fori_loop(0, T // TB, enter, 0)
+    if comm:
+        ag_a.go()
+        ag_b.go()
+        for g in rest:
+            g.go()
+        ag_a.go()
+        ag_b.go()
+        for g in rest:
+            g.go()
+        ag_a.go()
+        ag_b.go()
+        ag_a.go()
+        ag_b.go()
+        for g in rest:
+            g.go()
+        ag_a.go()
+        ag_b.go()
+    else:
+        for copy in loads[2:]:
+            copy.wait()
+
+    def first(i, _):
+        r = rows(i, TB)
+        proj[r, :] = dot(ctx[r, :], wide(qkv_cols)).astype(BF16)
         return 0
 
     lax.fori_loop(0, T // TB, first, 0)
@@ -105,79 +271,100 @@
             qaug[b * 2 * QB:b * 2 * QB + QB, :128] = jnp.where(low_lane, q, jnp.zeros_like(q))
             qaug[b * 2 * QB + QB:(b + 1) * 2 * QB, :128] = jnp.where(low_lane, jnp.zeros_like(q), q)
 
+    def ticks(p, plan):
+        for at, chains in plan.items():
+            @pl.when(p == at)
+            def _():
+                for chain in chains:
+                    chain.go()
+
+    plan = {1: (ag_up, ag_out), 2: (ag_down, ag_head), 4: (ag_up, ag_out), 5: (ag_down, ag_head)} if comm else {}
+
     def attend(p, _):
         stage_pair(p)
-        vt[...] = proj[:, slab(p, 2)].T
+        kt[...] = proj[:, slab(p, 2)].T
         for b in range(T // QB):
             low, high = window(b)
             s = dot_t(kaug[low:high, :], qaug[b * 2 * QB:(b + 1) * 2 * QB, :])
             top = jnp.max(s, axis=0, keepdims=True)
             e = jnp.exp(s - top)
             total = jnp.sum(e, axis=0, keepdims=True)
-            r = dot(vt[:, low:high], e.astype(BF16)) / total
+            r = dot(kt[:, low:high], e.astype(BF16)) / total
             c = jnp.where(low_row, r[:, :QB], r[:, QB:])
             lse[p, b:b + 1, :] = top + jnp.log(total)
             ctxt[pl.ds(pl.multiple_of(p * 128, 128), 128), b * QB:(b + 1) * QB] = c.astype(BF16)
             ctx[b * QB:(b + 1) * QB, slab(p, 0)] = c.T.astype(BF16)
+        ticks(p, plan)
         return 0
 
     lax.fori_loop(0, H // 2, attend, 0)
-    loads[1].wait()
+    if comm:
+        ag_up.finish()
+        ag_out.finish()
+
+    def block_of(ref, j, i):
+        return (j // 2, j % 2, lax.div(i, 2), lax.rem(i, 2))
 
     def up(i, _):
         r = rows(i, TB)
-        mid = x_ref[r, :].astype(F32) + dot(ctx[r, :], wa[:, 3 * D:4 * D])
+        mid = x_ref[r, :].astype(F32) + dot(ctx[r, :], wide(out_cols))
         xg_ref[r, :] = mid
         hat, _inv = norm_parts(mid)
         h2 = (hat * gain_ref[1:2, :] + shift_ref[1:2, :]).astype(BF16)
-        h2t[:, r] = h2.T
-
+        h2t[(*everywhere, ALL, r)] = h2.T.reshape(*FIVE, 24, TB)
         for j in range(FF // FB):
-            c = slice(j * FB, (j + 1) * FB)
-            pre = dot(h2, wm[0, :, c])
+            pre = dot(h2, tall(0, j))
             cdf = 0.5 * (1.0 + lax.erf(pre * 0.7071067811865476))
             pdf = jnp.exp(-0.5 * pre * pre) * 0.3989422804014327
-            hid[r, c] = (pre * cdf).astype(BF16)
-            gpre[r, c] = (cdf + pre * pdf).astype(BF16)
+            hid[block_of(hid, j, i)] = (pre * cdf).astype(BF16).reshape(2, 128, FB)
+            gpre[block_of(gpre, j, i)] = (cdf + pre * pdf).astype(BF16).reshape(2, 128, FB)
         return 0
 
     lax.fori_loop(0, T // TB, up, 0)
-    loads[2].wait()
-    loads[3].wait()
+    loads[0].wait()
+    loads[1].wait()
+    if comm:
+        ag_down.finish()
+        ag_head.finish()
     head_of = (lax.broadcasted_iota(jnp.int32, (16, D), 1) // HD
                == lax.broadcasted_iota(jnp.int32, (16, D), 0)).astype(BF16)
 
     def down(i, _):
         r = rows(i, TB)
         mid = xg_ref[r, :]
-        out = mid + dot_t(hid[r, :], wm[1])
+        out = mid
+        for j in range(FF // FB):
+            out = out + dot_t(hid[block_of(hid, j, i)].reshape(TB, FB), tall(1, j))
         hat, inv = norm_parts(out)
         h3 = (hat * gain_ref[2:3, :] + shift_ref[2:3, :]).astype(BF16)
-        h3t[:, r] = h3.T
-        al = dot(h3, wa[:, 4 * D:])
-        t = tg[r, :].astype(F32)
+        h3t[(*everywhere, ALL, r)] = h3.T.reshape(*FIVE, 24, TB)
+        al = dot(h3, wide(head_cols))
+        blk = (lax.div(i, 2), lax.rem(i, 2))
+        t = tg[blk].reshape(TB, TD).astype(F32)
         ra = lax.rsqrt(jnp.mean(al * al, axis=-1, keepdims=True) + eps_norm)
         rt = lax.rsqrt(jnp.mean(t * t, axis=-1, keepdims=True) + eps_norm)
         c = jnp.mean(al * t, axis=-1, keepdims=True)
         gal = (-(ra * rt) * (t - c * ra * ra * al)).astype(BF16)
-        tg[r, :] = gal
-        g3 = dot_t(gal, wa[:, 4 * D:])
+        tg[blk] = gal.reshape(2, 2, 2, 32, TD)
+        g3 = dot_t(gal, wide(head_cols))
         small_ref[2:3, :] += jnp.sum(g3 * hat, axis=0, keepdims=True)
         small_ref[5:6, :] += jnp.sum(g3, axis=0, keepdims=True)
         gout = cot[r, :].astype(F32) + norm_back(g3, hat, inv, gain_ref[2:3, :])
         cot[r, :] = out.astype(BF16)
         low = gout.astype(BF16)
-        got[:, r] = low.T
+        got[(*everywhere, ALL, r)] = low.T.reshape(*FIVE, 24, TB)
+        g2 = jnp.zeros((TB, D), F32)
         for j in range(FF // FB):
-            c = slice(j * FB, (j + 1) * FB)
-            gpre[r, c] = (dot(low, wm[1, :, c]) * gpre[r, c].astype(F32)).astype(BF16)
-        g2 = dot_t(gpre[r, :], wm[0])
+            at = block_of(gpre, j, i)
+            gp = (dot(low, tall(1, j)) * gpre[at].reshape(TB, FB).astype(F32)).astype(BF16)
+            gpre[at] = gp.reshape(2, 128, FB)
+            g2 = g2 + dot_t(gp, tall(0, j))
         hat2, inv2 = norm_parts(mid)
         small_ref[1:2, :] += jnp.sum(g2 * hat2, axis=0, keepdims=True)
         small_ref[4:5, :] += jnp.sum(g2, axis=0, keepdims=True)
         gmid = gout + norm_back(g2, hat2, inv2, gain_ref[1:2, :])
         xg_ref[r, :] = gmid
-        gc = dot_t(gmid.astype(BF16), wa[:, 3 * D:4 * D]).astype(BF16)
+        gc = dot_t(gmid.astype(BF16), wide(out_cols)).astype(BF16)
         e = ctx[r, :].astype(F32) * gc.astype(F32)
         e_high = e.astype(BF16)
         sums = dot_t(head_of, e_high) + dot_t(head_of, (e - e_high.astype(F32)).astype(BF16))
@@ -190,16 +377,63 @@
     y_copy = pltpu.make_async_copy(cot, y_hbm, sem.at[0])
     y_copy.start()
 
-    wa[:, 4 * D:] = dot(h3t[...], tg[...]).astype(BF16)
-
-    def ffgrad(j, _):
-        c = rows(j, GB)
-        wm[1, :, c] = dot(got[...], hid[:, c]).astype(BF16)
-        wm[0, :, c] = dot(h2t[...], gpre[:, c]).astype(BF16)
-        return 0
-
-    lax.fori_loop(0, FF // GB, ffgrad, 0)
-    wa[:, 3 * D:4 * D] = dot(ctxt[...], xg_ref[...].astype(BF16)).astype(BF16)
+    if comm:
+        xyz, yxz = (C, X, Y, Z1, Z2), (C, Y, X, Z1, Z2)
+        leads = ((0,), (1, 0), (1, 1, 0), (1, 1, 1, 0), (1, 1, 1, 1, 0))
+
+        def inside(ref, row, col):
+            return [Piece(ref, lead, row, col) for lead in leads]
+
+        def scatter(k, piece, order, lands, out):
+            return Scatter(place, piece, order, lands, rs_send.at[k], rs_recv.at[k], out)
+
+        def into(ref, at):
+            def put(value):
+                ref[at] = value
+            return put
+
+        low96, low24 = slice(0, 96), slice(96, 120)
+        rs_down = scatter(0, Piece(wm, (1,), ALL, ALL), xyz, inside(hid, low96, ALL), into(gm_out, 1))
+        rs_up = scatter(1, Piece(wm, (0,), ALL, ALL), yxz, inside(gpre, low96, ALL), into(gm_out, 0))
+        rs_head = scatter(2, Piece(wa, (), ALL, head_cols), yxz, inside(h3t, ALL, ALL),
+                          into(ga_out, (ALL, head_cols)))
+        rs_out = scatter(3, Piece(wa, (), ALL, out_cols), xyz, inside(hid, low24, ALL), into(ga_out, (ALL, out_cols)))
+        rs_qkv = []
+        for k in range(3):
+            cols = slice(k * D, (k + 1) * D)
+            rs_qkv.append(scatter(4 + k, Piece(gq, (), ALL, cols), xyz if k % 2 else yxz,
+                                  inside((h2t, got, tg)[k], slice(0, 24), slice(0, D)), into(ga_out, (ALL, cols))))
+
+        def meet(k):
+            for bit in range(5):
+                pl.semaphore_signal(ready.at[k], inc=1, device_id=place.partner(bit), device_id_type=pl.DeviceIdType.MESH)
+            pl.semaphore_wait(ready.at[k], 5)
+
+    def fold(ref, m, lhs):
+        def part(j, _):
+            a, b = lax.div(j, 2), lax.rem(j, 2)
+            g = dot(lhs[...].reshape(D, T), ref[a, b].reshape(T, FB)).astype(BF16)
+            wm[m, :, :, :, a, b] = g.reshape(2, 2, 2, 96, FB)
+            return 0
+
+        lax.fori_loop(0, FF // FB, part, 0)
+
+    wa[(*everywhere, ALL, head_cols)] = dot(h3t[...].reshape(D, T), tg[...].reshape(T, TD)).astype(BF16).reshape(*FIVE, 24, TD)
+    fold(hid, 1, got)
+    if comm:
+        meet(0)
+        rs_down.go()
+        rs_head.go()
+    wa[(*everywhere, ALL, out_cols)] = dot(ctxt[...], xg_ref[...].astype(BF16)).astype(BF16).reshape(*FIVE, 24, D)
+    if comm:
+        rs_out.go()
+        rs_down.go()
+    fold(gpre, 0, h2t)
+    if comm:
+        meet(1)
+        rs_up.go()
+        rs_head.go()
+        plan = {0: (rs_up, rs_out), 1: (rs_down, rs_head), 2: (rs_up, rs_out), 3: (rs_down, rs_head), 4: (rs_up, rs_out), 5: (rs_down, rs_head)}
 
     def attend_back(p, _):
         stage_pair(p)
@@ -230,16 +464,23 @@
             proj[qs, slab(p, 0)] = c.T.astype(BF16)
         proj[:, slab(p, 1)] = gka[...].astype(BF16)
         proj[:, slab(p, 2)] = gva[...].astype(BF16)
+        ticks(p, plan)
         return 0
 
     lax.fori_loop(0, H // 2, attend_back, 0)
 
-    for j in range(3):
-        gq[:, j * D:(j + 1) * D] = dot(h1t[...], proj[:, j * D:(j + 1) * D]).astype(BF16)
+    for k in range(3):
+        cols = slice(k * D, (k + 1) * D)
+        gq[(*everywhere, ALL, cols)] = dot(h1t[...], proj[:, cols]).astype(BF16).reshape(*FIVE, 24, D)
+        if comm:
+            rs_qkv[k].go()
+    if comm:
+        rs_up.go()
+        rs_out.go()
 
     def last(i, _):
         r = rows(i, TB)
-        g1 = dot_t(proj[r, :], wa[:, :3 * D])
+        g1 = dot_t(proj[r, :], wide(qkv_cols))
         hat, inv = norm_parts(x_ref[r, :].astype(F32))
         small_ref[0:1, :] += jnp.sum(g1 * hat, axis=0, keepdims=True)
         small_ref[3:4, :] += jnp.sum(g1, axis=0, keepdims=True)
@@ -248,37 +489,94 @@
 
     lax.fori_loop(0, T // TB, last, 0)
     y_copy.wait()
-    stores = []
-    for i, (src, dst) in enumerate(((gq, ga_hbm.at[:, :3 * D]), (wa.at[:, 3 * D:], ga_hbm.at[:, 3 * D:]), (wm, gm_hbm))):
-        copy = pltpu.make_async_copy(src, dst, sem.at[i])
-        copy.start()
-        stores.append(copy)
-    for copy in stores:
-        copy.wait()
-
-
-def compute(x, seg, gain, shift, tgt, cot, wa, wm):
+    if comm:
+        total = Total(place, small_ref, sm_land, sm_send, sm_recv)
+        for k in range(6):
+            total.go()
+            for chain in (*rs_qkv, rs_down, rs_head, rs_up, rs_out):
+                if chain.step < 5:
+                    chain.go()
+    else:
+        stores = [pltpu.make_async_copy(src, dst, sem.at[i]) for i, (src, dst) in enumerate((
+            (gq, ga_out.at[(*everywhere, ALL, qkv_cols)]),
+            (wa.at[(*everywhere, ALL, slice(3 * D, 4 * D + TD))], ga_out.at[(*everywhere, ALL, slice(3 * D, 4 * D + TD))]),
+            (wm, gm_out)))]
+        for copy in stores:
+            copy.start()
+        for copy in stores:
+            copy.wait()
+
+
+def compute(comm, x, seg, gain, shift, tgt, cot, wa, wm):
     vmem = pl.BlockSpec(memory_space=pltpu.VMEM)
     hbm = pl.BlockSpec(memory_space=pl.ANY)
     sds = jax.ShapeDtypeStruct
+    dma = pltpu.SemaphoreType.DMA
+    cols = 4 * D + TD
+    scratch = [
+        pltpu.VMEM((*FIVE, 24, cols), BF16), pltpu.VMEM((2, *FIVE, 96, FB), BF16), pltpu.VMEM((*FIVE, 24, 3 * D), BF16),
+        pltpu.VMEM((T, 3 * D), BF16), pltpu.VMEM((D, T), BF16), pltpu.VMEM((D, T), BF16),
+        pltpu.VMEM((*FIVE, 24, T), BF16), pltpu.VMEM((*FIVE, 24, T), BF16), pltpu.VMEM((*FIVE, 24, T), BF16),
+        pltpu.VMEM((*FIVE, 128, FB), BF16), pltpu.VMEM((*FIVE, 128, FB), BF16), pltpu.VMEM((*FIVE, 32, TD), BF16),
+        pltpu.VMEM((T, D), BF16), pltpu.VMEM((T, D), BF16),
+        pltpu.VMEM((T, 256), BF16), pltpu.VMEM((2 * T, 256), BF16), pltpu.VMEM((128, T), BF16),
+        pltpu.VMEM((T, 128), F32), pltpu.VMEM((T, 128), F32), pltpu.VMEM((H // 2, T // QB, 2 * QB), F32),
+        pltpu.VMEM((H, 1, T), F32), dma((4,)),
+    ]
+    if comm:
+        scratch += [dma((6, 5)), dma((6, 5)), dma((7, 5)), dma((7, 5)), pltpu.SemaphoreType.REGULAR((2,)), dma((5,)), dma((5,)),
+                    pltpu.VMEM((5, 8, D), F32)]
+        out_w = (sds((24, cols), F32), sds((2, 96, FB), F32))
+        params = pltpu.CompilerParams(vmem_limit_bytes=67043328, collective_id=0, has_side_effects=True)
+    else:
+        out_w = (sds((*FIVE, 24, cols), BF16), sds((2, *FIVE, 96, FB), BF16))
+        params = pltpu.CompilerParams(vmem_limit_bytes=67043328)
+    w = vmem if comm else hbm
     return pl.pallas_call(
-        compute_kernel,
-        out_shape=(sds((T, D), BF16), sds((T, D), F32), sds((D, 4 * D + TD), BF16), sds((2, D, FF), BF16), sds((8, D), F32)),
-        in_specs=[vmem, vmem, vmem, vmem, hbm, hbm, hbm, hbm],
-        out_specs=(hbm, vmem, hbm, hbm, vmem),
-        scratch_shapes=[
-            pltpu.VMEM((D, 4 * D + TD), BF16), pltpu.VMEM((2, D, FF), BF16), pltpu.VMEM((D, 3 * D), BF16),
-            pltpu.VMEM((T, 3 * D), BF16), pltpu.VMEM((D, T), BF16), pltpu.VMEM((D, T), BF16),
-            pltpu.VMEM((D, T), BF16), pltpu.VMEM((D, T), BF16), pltpu.VMEM((D, T), BF16),
-            pltpu.VMEM((T, FF), BF16), pltpu.VMEM((T, FF), BF16), pltpu.VMEM((T, TD), BF16),
-            pltpu.VMEM((T, D), BF16), pltpu.VMEM((T, D), BF16),
-            pltpu.VMEM((T, 256), BF16), pltpu.VMEM((2 * T, 256), BF16), pltpu.VMEM((128, T), BF16), pltpu.VMEM((128, T), BF16),
-            pltpu.VMEM((T, 128), F32), pltpu.VMEM((T, 128), F32), pltpu.VMEM((H // 2, T // QB, 2 * QB), F32),
-            pltpu.VMEM((H, 1, T), F32), pltpu.SemaphoreType.DMA((4,)),
-        ],
-        compiler_params=pltpu.CompilerParams(vmem_limit_bytes=67043328),
+        functools.partial(step_kernel, comm),
+        out_shape=(sds((T, D), BF16), sds((T, D), F32), *out_w, sds((8, D), F32)),
+        in_specs=[vmem, vmem, vmem, vmem, hbm, hbm, w, w],
+        out_specs=(hbm, vmem, w, w, vmem),
+        scratch_shapes=scratch,
+        compiler_params=params,
         name="block_step",
-    )(x, seg, gain, shift, tgt, cot, wa, wm)
+    )(x, seg, gain, shift, tgt.reshape(*FIVE, 32, TD), cot, wa, wm)
+
+
+def stats_kernel(n_dp, n_mp, in_ref, out_ref, land, send, recv):
+    dp, mp = lax.axis_index("dp"), lax.axis_index("mp")
+    partners, size = [], 1
+    while size < n_mp:
+        partners.append({"dp": dp, "mp": mp + size * (1 - 2 * lax.rem(lax.div(mp, size), 2))})
+        size *= 2
+    size = 1
+    while size < n_dp:
+        partners.append({"dp": dp + size * (1 - 2 * lax.rem(lax.div(dp, size), 2)), "mp": mp})
+        size *= 2
+    barrier = pltpu.get_barrier_semaphore()
+    for other in partners:
+        pl.semaphore_signal(barrier, inc=1, device_id=other, device_id_type=pl.DeviceIdType.MESH)
+    out_ref[...] = in_ref[...]
+    pl.semaphore_wait(barrier, len(partners))
+    for j, other in enumerate(partners):
+        copy = pltpu.make_async_remote_copy(out_ref, land.at[j], send.at[j], recv.at[j], device_id=other, device_id_type=pl.DeviceIdType.MESH)
+        copy.start()
+        copy.wait()
+        out_ref[...] = out_ref[...] + land[j]
+
+
+def all_sum(value, n_dp, n_mp):
+    bits = (n_dp * n_mp).bit_length() - 1
+    vmem = pl.BlockSpec(memory_space=pltpu.VMEM)
+    return pl.pallas_call(
+        functools.partial(stats_kernel, n_dp, n_mp),
+        out_shape=jax.ShapeDtypeStruct(value.shape, F32),
+        in_specs=[vmem],
+        out_specs=vmem,
+        scratch_shapes=[pltpu.VMEM((bits, *value.shape), F32), pltpu.SemaphoreType.DMA((bits,)), pltpu.SemaphoreType.DMA((bits,))],
+        compiler_params=pltpu.CompilerParams(collective_id=1, has_side_effects=True),
+        name="stats_sum",
+    )(value)
 
 
 def moments(weight, gradient, first_old, second_old, wd_rate):
@@ -291,6 +589,8 @@
 
 
 def on_device(
+    n_dp,
+    n_mp,
     x_in,
     segments,
     targets,
@@ -306,16 +606,24 @@
     mlp_first,
     mlp_second,
 ):
-    w_attn = lax.all_gather(attn_w.astype(BF16), ("dp", "mp"), axis=0, tiled=True)
-    w_mlp = lax.all_gather(mlp_w.astype(BF16), "dp", axis=1, tiled=True)
-    w_mlp = lax.all_gather(w_mlp, "mp", axis=2, tiled=True)
-    y_out, grad_in, part_attn, part_mlp, part_small = compute(
-        x_in, segments, norm_gain, norm_bias, targets, cotangent, w_attn, w_mlp
-    )
-    grad_mlp = lax.psum_scatter(part_mlp, "dp", scatter_dimension=1, tiled=True)
-    grad_mlp = lax.psum_scatter(grad_mlp, "mp", scatter_dimension=2, tiled=True).astype(F32)
-    grad_attn = lax.psum_scatter(part_attn, ("dp", "mp"), scatter_dimension=0, tiled=True).astype(F32)
-    small_grad = lax.psum(part_small[:6], ("dp", "mp"))
+    if n_dp == 8 and n_mp == 4:
+        y_out, grad_in, grad_attn, grad_mlp, small_grad = compute(
+            True, x_in, segments, norm_gain, norm_bias, targets, cotangent, attn_w, mlp_w
+        )
+        small_grad = small_grad[:6]
+    else:
+        w_attn = lax.all_gather(attn_w.astype(BF16), ("dp", "mp"), axis=0, tiled=True)
+        w_mlp = lax.all_gather(mlp_w.astype(BF16), "dp", axis=1, tiled=True)
+        w_mlp = lax.all_gather(w_mlp, "mp", axis=2, tiled=True)
+        y_out, grad_in, part_attn, part_mlp, part_small = compute(
+            False, x_in, segments, norm_gain, norm_bias, targets, cotangent, w_attn.reshape(*FIVE, 24, -1),
+            w_mlp.reshape(2, 8, 96, 4, FB).transpose(0, 1, 3, 2, 4).reshape(2, *FIVE, 96, FB)
+        )
+        part_mlp = part_mlp.reshape(2, 8, 4, 96, FB).transpose(0, 1, 3, 2, 4).reshape(2, D, FF)
+        grad_mlp = lax.psum_scatter(part_mlp, "dp", scatter_dimension=1, tiled=True)
+        grad_mlp = lax.psum_scatter(grad_mlp, "mp", scatter_dimension=2, tiled=True).astype(F32)
+        grad_attn = lax.psum_scatter(part_attn.reshape(D, -1), ("dp", "mp"), scatter_dimension=0, tiled=True).astype(F32)
+        small_grad = lax.psum(part_small[:6], ("dp", "mp"))
     attn_first_new, attn_second_new, attn_update = moments(
         attn_w, grad_attn, attn_first, attn_second, decay_rate
     )
@@ -343,7 +651,7 @@
         ]
     )
     local_stats = jnp.stack([weight_sq, update_sq])
-    totals = lax.psum(local_stats, ("dp", "mp"))
+    totals = all_sum(jnp.pad(local_stats, ((0, 6), (0, 123))), n_dp, n_mp)[:2, :5]
     lamb_norms = jnp.sqrt(totals)
     ratio = lamb_norms[0] / lamb_norms[1]
     ratio_cols = jnp.concatenate(
@@ -391,7 +699,7 @@
         P(None, "dp", "mp"),
     )
     return jax.shard_map(
-        on_device,
+        functools.partial(on_device, mesh.shape["dp"], mesh.shape["mp"]),
         mesh=mesh,
         in_specs=placed,
         out_specs=(

time: 710 us -> 309 us (0.44)
  waiting for transfers between devices: 491 us -> 0 us
  Pallas kernels: 137 us -> 279 us
  blocking collectives: 39.7 us -> 0 us
  between operations: 15.7 us -> 2.22 us
    reduce_scatter x3 -> x0, waiting for transfers between devices: 301 us -> none  [the longest x1 162 us: on_device(): grad_mlp = lax.psum_scatter(part_mlp, 'dp', scatter_dimension=1, tiled=True)]
    all_gather x3 -> x0, waiting for transfers between devices: 190 us -> none  [the longest x1 71.2 us: on_device(): lax.all_gather(attn_w.astype(BF16), ('dp', 'mp'), axis=0, tiled=True)]
    pallas_call x1 -> x2, Pallas kernels: 137 us -> 279 us  [the longest x1 265 us: compute(): pl.pallas_call(functools.partial(step_kernel, comm), out_shape=(sds((T, D...]
    psum x1 -> x0, blocking collectives: 39.7 us -> none  [on_device(): totals = lax.psum(local_stats, ('dp', 'mp'))]
  transfers between devices with their start and end apart: 6 -> 0, of which waited for: 6 -> 0; matrix products, arithmetic and copies ran while one was open for 1% -> 0% of each run, Pallas kernels for 0% -> 0%
where the time goes in v2:
time: 309 us; the launch traced here: 308 us
  Pallas kernels  279 us (90%)
  local copies, waits for them, and re-layouts  14 us (5%)
  other arithmetic  12.8 us (4%)
    pallas_call x1, Pallas kernels, compute(): pl.pallas_call(functools.partial(step_kernel, comm), out_shape=(sds((T, D...  265 us
    pallas_call x1, Pallas kernels, all_sum(): pl.pallas_call(functools.partial(stats_kernel, n_dp, n_mp), out_shape=jax...  14.1 us

profile of v2, /device:TPU:0, one launch (start us, length us, event | category | flops | bytes accessed | tf_op | source)
XLA Modules:
  0.0 308.3 jit_solution(1516522125596941473)
XLA Ops:
  0.6 265.2 %block_step.1 = (bf16[1024,768]{1,0:T(8,128)(2,1)}, f32[1024,768]{1,0:T(8,128)}, f32[24,4096]{1,0:T(8,128)}, f32[2,96,768]{2,1,0:T(8,128)}, f32[8,768]{1,0:T(8,128)}) custom-call(bf16[1024,768]{1,0:T(8,128)(2,1)} %refs_0_.1, s32[1,1024]{1,0:T(1,128)} %refs_1_.1, f32[3,768]{1,0:T(4,128)} %refs_2_.1, f32[3,768]{1,0:T(4,128)} %refs_3_.1, ...), custom_call_target="tpu_custom_call" | custom-call | tf_op jit(solution)/shard_map/block_step/pallas_call | solution.py:535
  265.8 0.0 copy-start
  265.8 0.0 copy-start.5
  265.9 0.0 copy-start.6
  265.9 2.6 multiply_reduce_fusion.1
  268.5 0.6 slice_reduce_fusion
  269.1 0.6 slice_reduce_fusion.3
  269.7 0.6 slice_reduce_fusion.2
  270.3 1.4 multiply_add_fusion
  271.7 0.7 fusion.2
  272.4 3.3 %stack.57 = f32[5]{0:T(128)S(1)} concatenate(f32[1]{0:T(128)} %bitcast.7, f32[1]{0:T(128)} %bitcast.8, f32[1]{0:T(128)} %bitcast.9, f32[1]{0:T(128)} %bitcast.10, f32[1]{0:T(128)} %bitcast.11), dimensions={0} | concatenate | bytes 40 | tf_op jit(solution)/shard_map/stack | solution.py:644
  275.7 0.7 multiply_reduce_fusion.2
  276.4 3.3 %stack.50 = f32[5]{0:T(128)S(1)} concatenate(f32[1]{0:T(128)} %bitcast.1, f32[1]{0:T(128)} %bitcast.2, f32[1]{0:T(128)} %bitcast.3, f32[1]{0:T(128)} %bitcast.4, f32[1]{0:T(128)} %bitcast.5), dimensions={0} | concatenate | bytes 40 | tf_op jit(solution)/shard_map/stack | solution.py:635
  279.7 0.6 select_maximum_fusion.in_ref
  280.3 14.1 %stats_sum.1 = f32[8,128]{1,0:T(8,128)} custom-call(f32[8,128]{1,0:T(8,128)} %select_maximum_fusion.in_ref), custom_call_target="tpu_custom_call" | custom-call | tf_op jit(solution)/shard_map/stats_sum/pallas_call | solution.py:571
  294.4 0.7 slice_sqrt_fusion
  295.1 0.6 fusion.8
  295.7 0.6 broadcast_in_dim.13
  296.4 0.6 broadcast_in_dim.12
  297.0 0.6 broadcast_in_dim.11
  297.7 0.0 copy-start.8
  297.7 0.0 copy-start.9
  297.8 0.0 copy-start.11
  297.8 0.0 copy-start.12
  297.8 2.1 multiply_subtract_fusion.1
  299.9 0.1 multiply_bitcast_fusion
  300.0 0.9 multiply_subtract_fusion
  300.9 1.2 multiply_reduce_fusion.4
  303.6 0.6 multiply_subtract_fusion.2
  304.2 1.1 copy.28
  305.3 1.3 copy-done.2
  306.6 1.7 copy.29
  (24 shorter events, 0.1 us)
Async XLA Ops:
  265.8 4.5 %copy-start = (f32[2,96,768]{2,1,0:T(8,128)S(1)}, f32[2,96,768]{2,1,0:T(8,128)}, u32[]{:S(2)}) copy-start(f32[2,96,768]{2,1,0:T(8,128)} %refs_7_.1) | copy-start | bytes 1769476
  265.8 4.5 %copy-start.5 = (f32[2,96,768]{2,1,0:T(8,128)S(1)}, f32[2,96,768]{2,1,0:T(8,128)}, u32[]{:S(2)}) copy-start(f32[2,96,768]{2,1,0:T(8,128)} %param.26) | copy-start | bytes 1769476
  265.9 4.5 %copy-start.6 = (f32[2,96,768]{2,1,0:T(8,128)S(1)}, f32[2,96,768]{2,1,0:T(8,128)}, u32[]{:S(2)}) copy-start(f32[2,96,768]{2,1,0:T(8,128)} %param.27) | copy-start | bytes 1769476
  265.9 4.5 %copy-start.7 = (f32[2,96,768]{2,1,0:T(8,128)S(1)}, f32[2,96,768]{2,1,0:T(8,128)}, u32[]{:S(2)}) copy-start(f32[2,96,768]{2,1,0:T(8,128)} %get-tuple-element.20) | copy-start | bytes 1769476
  268.5 29.2 %copy-start.4 = (f32[24,4096]{1,0:T(8,128)}, f32[24,4096]{1,0:T(8,128)S(1)}, u32[]{:S(2)}) copy-start(f32[24,4096]{1,0:T(8,128)S(1)} %get-tuple-element.62) | copy-start | bytes 1179652
  271.7 26.0 %copy-start.1 = (f32[24,4096]{1,0:T(8,128)S(1)}, f32[24,4096]{1,0:T(8,128)}, u32[]{:S(2)}) copy-start(f32[24,4096]{1,0:T(8,128)} %refs_6_.1) | copy-start | bytes 1179652
  295.1 5.8 %copy-start.14 = (f32[2,5]{1,0:T(2,128)}, f32[2,5]{1,0:T(2,128)S(1)}, u32[]{:S(2)}) copy-start(f32[2,5]{1,0:T(2,128)S(1)} %slice_sqrt_fusion) | copy-start | bytes 124
  297.7 3.2 %copy-start.8 = (f32[3,768]{1,0:T(4,128)S(1)}, f32[3,768]{1,0:T(4,128)}, u32[]{:S(2)}) copy-start(f32[3,768]{1,0:T(4,128)} %refs_2_.1) | copy-start | bytes 27652
  297.7 3.2 %copy-start.9 = (f32[3,768]{1,0:T(4,128)S(1)}, f32[3,768]{1,0:T(4,128)}, u32[]{:S(2)}) copy-start(f32[3,768]{1,0:T(4,128)} %refs_3_.1) | copy-start | bytes 27652
  297.8 3.2 %copy-start.11 = (f32[6,768]{1,0:T(8,128)S(1)}, f32[6,768]{1,0:T(8,128)}, u32[]{:S(2)}) copy-start(f32[6,768]{1,0:T(8,128)} %param.22) | copy-start | bytes 55300
  297.8 3.1 %copy-start.12 = (f32[6,768]{1,0:T(8,128)S(1)}, f32[6,768]{1,0:T(8,128)}, u32[]{:S(2)}) copy-start(f32[6,768]{1,0:T(8,128)} %param.23) | copy-start | bytes 55300
  297.8 3.1 %copy-start.13 = (f32[8,768]{1,0:T(8,128)S(1)}, f32[8,768]{1,0:T(8,128)}, u32[]{:S(2)}) copy-start(f32[8,768]{1,0:T(8,128)} %get-tuple-element.21) | copy-start | bytes 73732
  297.8 6.4 %copy-start.3 = (bf16[1024,768]{1,0:T(8,128)(2,1)S(1)}, bf16[1024,768]{1,0:T(8,128)(2,1)}, u32[]{:S(2)}) copy-start(bf16[1024,768]{1,0:T(8,128)(2,1)} %get-tuple-element.59) | copy-start | bytes 4718596
  299.9 3.7 %copy-start.10 = (f32[3,768]{1,0:T(4,128)S(1)}, f32[3,768]{1,0:T(4,128)}, u32[]{:S(2)}) copy-start(f32[3,768]{1,0:T(4,128)} %refs_3_.1) | copy-start | bytes 27652
  304.2 2.5 copy-start.2
